TPU v7x, 32 devices: a 4x4x1 block of a 4x4x8 slice. The times are simulated.
32 devices in a mesh: dp: 1 (over z), ty: 4 (over y), tx: 8 (over x, core).
Axes of the slice: x: 4, y: 4, z: 1, core: 2. Of those that a mesh axis runs over, the one named last changes fastest.
The devices are a block of a 4x4x8 slice.
Arguments:
- x: bfloat16 [2048, 8192], P(('dp', 'ty'), 'tx')
- positions: int32 [2, 1024], P('dp')
- norm_gain: float32 [8192], P('tx')
- w_q: bfloat16 [8192, 8192], P('tx', 'ty')
- w_k: bfloat16 [8192, 1024], P('tx', 'ty')
- w_v: bfloat16 [8192, 1024], P('tx', 'ty')
- w_o: bfloat16 [8192, 8192], P('ty', 'tx')
- w_gate: bfloat16 [8192, 24576], P('tx', 'ty')
- w_up: bfloat16 [8192, 24576], P('tx', 'ty')
- w_down: bfloat16 [24576, 8192], P('ty', 'tx')
Outputs:
- output: bfloat16 [2048, 8192], P(('dp', 'ty'), 'tx')
All inputs are finite; a program needn't handle non-finite values.
Results may differ from a plain program's by a relative error of at most 0.0178161.
Values are sent between devices in bfloat16 or wider.
A program may use at most 768 MiB of HBM per device.

v0:
```python
import math
import jax
import jax.numpy as jnp
from jax import lax
from jax.sharding import PartitionSpec as P

HEAD = 128
WINDOW = 4096
ROPE_THETA = 50000
QBLOCK = 256


def rotary(heads_in, pos_ids):
    half_dim = HEAD // 2
    inv_freq = ROPE_THETA ** (-2.0 * jnp.arange(half_dim, dtype=jnp.float32) / HEAD)
    rot_angle = pos_ids.astype(jnp.float32)[:, None] * inv_freq[None, :]
    cos_a = jnp.cos(rot_angle)[:, None, :]
    sin_a = jnp.sin(rot_angle)[:, None, :]
    pair_vals = heads_in.astype(jnp.float32).reshape(heads_in.shape[:-1] + (half_dim, 2))
    even_part = pair_vals[..., 0]
    odd_part = pair_vals[..., 1]
    rotated = jnp.stack([even_part * cos_a - odd_part * sin_a, even_part * sin_a + odd_part * cos_a], axis=-1)
    return rotated.reshape(heads_in.shape).astype(jnp.bfloat16)


def band_attention(q_rot, k_rot, v_heads, q_first, seq_len):
    q_rows = q_rot.shape[0]
    tokens = k_rot.shape[0]
    q_block = math.gcd(q_rows, QBLOCK)
    band_len = min(tokens, q_block + min(WINDOW, seq_len))
    q_blocks = q_rot.reshape((q_rows // q_block, q_block) + q_rot.shape[1:])

    def one_block(blk_args):
        q_blk, blk_idx = blk_args
        q_start = q_first + blk_idx * q_block
        k_start = jnp.clip(q_start + q_block - band_len, 0, tokens - band_len)
        k_blk = lax.dynamic_slice_in_dim(k_rot, k_start, band_len, 0)
        v_blk = lax.dynamic_slice_in_dim(v_heads, k_start, band_len, 0)
        scores = jnp.einsum("qgrd,kgd->grqk", q_blk, k_blk, preferred_element_type=jnp.float32) * HEAD ** -0.5
        q_idx = q_start + jnp.arange(q_block)
        k_idx = k_start + jnp.arange(band_len)
        tok_gap = q_idx[:, None] - k_idx[None, :]
        allowed = (tok_gap >= 0) & (tok_gap < WINDOW) & (q_idx[:, None] // seq_len == k_idx[None, :] // seq_len)
        scores = jnp.where(allowed, scores, -1e30)
        row_max = jnp.max(scores, axis=-1, keepdims=True)
        exp_scores = jnp.exp(scores - row_max)
        row_total = jnp.sum(exp_scores, axis=-1)
        weighted = jnp.einsum("grqk,kgd->qgrd", exp_scores.astype(jnp.bfloat16), v_blk, preferred_element_type=jnp.float32)
        return (weighted / jnp.transpose(row_total, (2, 0, 1))[..., None]).astype(jnp.bfloat16)

    results = lax.map(one_block, (q_blocks, jnp.arange(q_rows // q_block)))
    return results.reshape(q_rows, -1)


def solution(mesh):
    tx_size = mesh.shape["tx"]
    ty_size = mesh.shape["ty"]

    def per_device(x_blk, positions, norm_gain, w_q, w_k, w_v, w_o, w_gate, w_up, w_down):
        d_model = x_blk.shape[1] * tx_size
        seq_len = positions.shape[1]
        x_wide = x_blk.astype(jnp.float32)
        tok_stats = lax.psum(jnp.stack([jnp.sum(x_wide, axis=1), jnp.sum(x_wide * x_wide, axis=1)], axis=1), "tx")
        tok_mean = tok_stats[:, :1] / d_model
        tok_var = tok_stats[:, 1:] / d_model - tok_mean * tok_mean
        normed = (norm_gain * (x_wide - tok_mean) * lax.rsqrt(tok_var + 1e-5)).astype(jnp.bfloat16)
        n_all = lax.all_gather(normed, "ty", axis=0, tiled=True)
        tokens = n_all.shape[0]
        q_rows = tokens // tx_size
        part_q = jnp.dot(n_all, w_q, preferred_element_type=jnp.float32).astype(jnp.bfloat16)
        part_rest = tuple(jnp.dot(n_all, w_mat, preferred_element_type=jnp.float32).astype(jnp.bfloat16)
                          for w_mat in (w_k, w_v, w_gate, w_up))
        q_proj = lax.psum_scatter(part_q, "tx", scatter_dimension=0, tiled=True)
        k_proj, v_proj, gate_act, up_act = lax.psum(part_rest, "tx")
        if w_k.shape[1] < HEAD:
            kv_total = w_k.shape[1] * ty_size // HEAD
            kv_index = lax.axis_index("ty") * kv_total // ty_size
            k_proj = lax.dynamic_slice_in_dim(lax.all_gather(k_proj, "ty", axis=1, tiled=True), kv_index * HEAD, HEAD, 1)
            v_proj = lax.dynamic_slice_in_dim(lax.all_gather(v_proj, "ty", axis=1, tiled=True), kv_index * HEAD, HEAD, 1)
        heads_loc = w_q.shape[1] // HEAD
        kv_loc = k_proj.shape[1] // HEAD
        pos_flat = positions.reshape(tokens)
        q_first = lax.axis_index("tx") * q_rows
        q_pos = lax.dynamic_slice_in_dim(pos_flat, q_first, q_rows, 0)
        q_rot = rotary(q_proj.reshape(q_rows, heads_loc, HEAD), q_pos).reshape(q_rows, kv_loc, heads_loc // kv_loc, HEAD)
        k_rot = rotary(k_proj.reshape(tokens, kv_loc, HEAD), pos_flat)
        v_heads = v_proj.reshape(tokens, kv_loc, HEAD)
        attn_rows = band_attention(q_rot, k_rot, v_heads, q_first, seq_len)
        attn_all = lax.all_gather(attn_rows, "tx", axis=0, tiled=True)
        hidden = (jax.nn.silu(gate_act.astype(jnp.float32)) * up_act.astype(jnp.float32)).astype(jnp.bfloat16)
        block_out = jnp.dot(attn_all, w_o, preferred_element_type=jnp.float32) + jnp.dot(hidden, w_down, preferred_element_type=jnp.float32)
        block_sum = lax.psum_scatter(block_out.astype(jnp.bfloat16), "ty", scatter_dimension=0, tiled=True)
        return (x_wide + block_sum.astype(jnp.float32)).astype(jnp.bfloat16)

    in_specs = (P(("dp", "ty"), "tx"), P("dp", None), P("tx"), P("tx", "ty"), P("tx", "ty"), P("tx", "ty"),
                P("ty", "tx"), P("tx", "ty"), P("tx", "ty"), P("ty", "tx"))
    return jax.shard_map(per_device, mesh=mesh, in_specs=in_specs, out_specs=P(("dp", "ty"), "tx"), check_vma=False)
```

profile of v0, /device:TPU:97, one launch (start us, length us, event | category | flops | bytes accessed | tf_op | source)
XLA Modules:
  0.0 863.2 jit_solution(8196019980684107159)
XLA Ops:
  6.5 0.0 copy-start
  6.6 0.0 all-gather.3.cloned.1.call-start
  6.6 1.7 convert_reduce_fusion
  8.2 13.9 %psum.35 = f32[512,2]{0,1:T(2,128)S(1)} all-reduce(f32[512,2]{0,1:T(2,128)S(1)} %pad_maximum_fusion.2), channel_id=1, replica_groups=mesh['dp'=1,'ty'=4,'tx'=8] {'tx'}, use_global_device_ids=true, to_apply=%region_2.0 | all-reduce | flops 1024 | bytes 8192 | tf_op jit(solution)/shard_map/psum | solution.py:63
  22.1 2.6 fusion.18
  24.7 0.1 all-gather.3.cloned.1.call-update
  24.8 0.1 reduce-scatter.3.cloned.1.call-start
  24.8 47.8 %all-gather.3.cloned.1.call-done = bf16[2048,1024]{1,0:T(8,128)(2,1)} async-done(((bf16[512,1024]{1,0:T(8,128)(2,1)}), bf16[2048,1024]{1,0:T(8,128)(2,1)}) %all-gather.3.cloned.1.call-update) | async-done | bytes 4194320 | tf_op jit(solution)/shard_map/all_gather | solution.py:67
  72.7 13.9 %convolution_convert_fusion.2 = bf16[2048,2048]{1,0:T(8,128)(2,1)} fusion(bf16[2048,1024]{1,0:T(8,128)(2,1)} %all-gather.3.cloned.1.call-done, bf16[1024,2048]{1,0:T(8,128)(2,1)} %param.13), kind=kOutput, calls=%fused_computation.18 | convolution fusion | flops 8594128896 | bytes 16777216 | tf_op jit(solution)/shard_map/dot_general | solution.py:70
  86.6 0.1 reduce-scatter.3.cloned.1.call-update
  86.6 0.0 copy-start.6
  86.7 0.5 all-reduce.3.cloned.1.call-start
  87.2 0.0 copy-done
  87.2 3.5 convolution_convert_fusion.3
  90.7 0.7 convert_element_type.84
  91.4 0.0 copy-start.4
  91.4 2.0 copy.14
  93.5 0.0 copy-done.6
  93.5 4.5 convolution_convert_fusion.4
  98.0 0.0 copy-done.4
  98.0 33.8 %convolution_convert_fusion = bf16[2048,6144]{1,0:T(8,128)(2,1)} fusion(bf16[2048,1024]{1,0:T(8,128)(2,1)S(1)} %copy-done.4, bf16[1024,6144]{1,0:T(8,128)(2,1)} %param.18), kind=kOutput, calls=%fused_computation.8 | convolution fusion | flops 25782386688 | bytes 41943040 | tf_op jit(solution)/shard_map/dot_general | solution.py:71
  131.8 33.8 %convolution_convert_fusion.1 = bf16[2048,6144]{1,0:T(8,128)(2,1)} fusion(bf16[2048,1024]{1,0:T(8,128)(2,1)S(1)} %copy-done.4, bf16[1024,6144]{1,0:T(8,128)(2,1)} %param.17), kind=kOutput, calls=%fused_computation.9 | convolution fusion | flops 25782386688 | bytes 41943040 | tf_op jit(solution)/shard_map/dot_general | solution.py:71
  165.6 0.0 copy-start.3
  165.6 0.1 all-reduce.3.cloned.1.call-update
  165.7 0.2 all-gather.5.cloned.1.call-start
  165.9 0.4 copy-done.3
  166.3 0.1 dynamic-slice_convert_fusion
  166.4 0.3 multiply_cosine_fusion.1
  166.7 0.9 fusion.24
  167.6 2.7 multiply_cosine_fusion
  170.3 0.0 reduce-scatter.3.cloned.1.call-done
  170.3 2.6 copy.16
  172.9 2.5 reshape.212
  175.4 2.9 subtract_convert_fusion
  178.3 2.4 pad_maximum_fusion.1
  180.7 1.1 copy.17
  181.9 496.6 %all-reduce.3.cloned.1.call-done = (bf16[2048,2,64,2]{0,1,3,2:T(2,128)(2,1)}, bf16[2048,2,128]{0,2,1:T(8,128)(2,1)}, bf16[2048,6144]{1,0:T(8,128)(2,1)}, bf16[2048,6144]{1,0:T(8,128)(2,1)}) async-done(((bf16[2048,2,64,2]{0,1,3,2:T(2,128)(2,1)}, bf16[2048,2,128]{0,2,1:T(8,128)(2,1)}, bf16[2048,6144]{1,0:T(8,128)(2,1)}, bf16[2048,6144]{1,0:T(8,128)(2,1)}), (bf16[2048,2,64,2]{0,1,3,2:T(2,128)(2,1)}, ...) | async-done | bytes 52428816 | tf_op jit(solution)/shard_map/psum | solution.py:74
  678.5 2.2 convert_element_type.85
  680.8 2.2 subtract_convert_fusion.1
  682.9 1.4 pad_maximum_fusion
  684.3 1.4 constant_dynamic-slice_fusion
  685.7 1.0 copy.23
  686.6 3.6 fusion.9
  690.2 0.0 copy-start.5
  690.2 4.4 fusion.7
  694.6 0.0 copy-done.5
  694.6 6.4 fusion.20
  701.0 0.1 all-gather.5.cloned.1.call-update
  701.0 0.1 reduce-scatter.5.cloned.1.call-start
  701.1 50.9 %all-gather.5.cloned.1.call-done = bf16[2048,2048]{0,1:T(8,128)(2,1)} async-done(((bf16[256,2048]{0,1:T(8,128)(2,1)}), bf16[2048,2048]{0,1:T(8,128)(2,1)}) %all-gather.5.cloned.1.call-update) | async-done | bytes 8388624 | tf_op jit(solution)/shard_map/all_gather | solution.py:89
  752.1 14.6 %fusion.39 = f32[2048,1024]{1,0:T(8,128)} fusion(bf16[2048,2048]{0,1:T(8,128)(2,1)} %all-gather.5.cloned.1.call-done, bf16[2048,1024]{1,0:T(8,128)(2,1)} %param.16), kind=kOutput, calls=%fused_computation.79 | convolution fusion | flops 8589934592 | bytes 20971520 | tf_op jit(solution)/shard_map/dot_general | solution.py:91
  766.6 0.0 copy-start.2
  766.6 0.0 copy-start.1
  766.6 42.3 %add_convert_fusion = bf16[2048,1024]{1,0:T(8,128)(2,1)} fusion(f32[2048,1024]{1,0:T(8,128)} %fusion.39, bf16[6144,1024]{1,0:T(8,128)(2,1)} %param.19, bf16[2048,6144]{1,0:T(8,128)(2,1)} %get-tuple-element.26, bf16[2048,6144]{1,0:T(8,128)(2,1)} %get-tuple-element.28), kind=kOutput, calls=%fused_computation.17 | convolution fusion | flops 25874661376 | bytes 75497472 | tf_op jit(solution)/shard_map/dot_general | solution.py:91
  809.0 0.1 reduce-scatter.5.cloned.1.call-update
  809.0 44.8 %reduce-scatter.5.cloned.1.call-done = bf16[512,1024]{1,0:T(8,128)(2,1)} async-done(((bf16[2048,1024]{1,0:T(8,128)(2,1)}), bf16[512,1024]{1,0:T(8,128)(2,1)}) %reduce-scatter.5.cloned.1.call-update) | async-done | bytes 1048592 | tf_op jit(solution)/shard_map/reduce_scatter | solution.py:92
  853.8 0.0 copy-done.2
  853.8 2.6 fusion.19
  856.4 0.0 copy-done.1
  (6 shorter events, 0.1 us)
Async XLA Ops:
  6.5 80.7 %copy-start = (bf16[1024,256]{1,0:T(8,128)(2,1)S(1)}, bf16[1024,256]{1,0:T(8,128)(2,1)}, u32[]{:S(2)}) copy-start(bf16[1024,256]{1,0:T(8,128)(2,1)} %param.14) | copy-start | bytes 1572868
  6.6 66.1 %all-gather.3.cloned.1.call-start = ((), (), s32[]{:S(2)}) async-start(), calls=%async_computation.2 | async-start | bytes 5242880 | tf_op jit(solution)/shard_map/all_gather | solution.py:67
  24.8 145.6 %reduce-scatter.3.cloned.1.call-start = ((), (), s32[]{:S(2)}) async-start(), calls=%async_computation.3 | async-start | bytes 9437184 | tf_op jit(solution)/shard_map/reduce_scatter | solution.py:73
  86.6 6.8 copy-start.6
  86.7 591.8 %all-reduce.3.cloned.1.call-start = ((), (), s32[]{:S(2)}) async-start(), calls=%async_computation.6 | async-start | bytes 104857600 | tf_op jit(solution)/shard_map/psum | solution.py:74
  91.4 6.6 copy-start.4
  165.6 0.7 copy-start.3
  165.7 586.4 %all-gather.5.cloned.1.call-start = ((), (), s32[]{:S(2)}) async-start(), calls=%async_computation.4 | async-start | bytes 9437184 | tf_op jit(solution)/shard_map/all_gather | solution.py:89
  690.2 4.4 copy-start.5
  701.0 152.8 %reduce-scatter.5.cloned.1.call-start = ((), (), s32[]{:S(2)}) async-start(), calls=%async_computation.5 | async-start | bytes 5242880 | tf_op jit(solution)/shard_map/reduce_scatter | solution.py:92
  766.6 87.2 %copy-start.2 = (bf16[512,1024]{1,0:T(8,128)(2,1)S(1)}, bf16[512,1024]{1,0:T(8,128)(2,1)}, u32[]{:S(2)}) copy-start(bf16[512,1024]{1,0:T(8,128)(2,1)} %param.10) | copy-start | bytes 3145732
  766.6 89.8 %copy-start.1 = (bf16[1024,256]{1,0:T(8,128)(2,1)S(1)}, bf16[1024,256]{1,0:T(8,128)(2,1)}, u32[]{:S(2)}) copy-start(bf16[1024,256]{1,0:T(8,128)(2,1)} %param.14) | copy-start | bytes 1572868
Sparse Core Ops, SparseCore 0:
  24.9 47.7 all-gather.2
  86.8 50.0 reduce-scatter.2
  165.8 512.6 all-reduce.2
  701.2 50.8 all-gather.4
  809.1 44.6 reduce-scatter.4
where the time goes:
time: 868 us; the launch traced here: 863 us
  waiting for transfers between devices  640 us (74%)
  matrix products  156 us (18%)
  other arithmetic  26.4 us (3%)
  blocking collectives  13.9 us (2%)
  between operations  13.6 us (2%)
  local copies, waits for them, and re-layouts  11.6 us (1%)
    psum x1, waiting for transfers between devices, per_device(): k_proj, v_proj, gate_act, up_act = lax.psum(part_rest, 'tx')  497 us
    dot_general x4, matrix products, per_device(): jnp.dot(n_all, w_mat, preferred_element_type=jnp.float32)  75.6 us
    all_gather x1, waiting for transfers between devices, per_device(): attn_all = lax.all_gather(attn_rows, 'tx', axis=0, tiled=True)  50.9 us
    all_gather x1, waiting for transfers between devices, per_device(): n_all = lax.all_gather(normed, 'ty', axis=0, tiled=True)  47.8 us
    reduce_scatter x1, waiting for transfers between devices, per_device(): lax.psum_scatter(block_out.astype(jnp.bfloat16), 'ty', scatter_dimension=...  44.8 us
    dot_general x1, matrix products, per_device(): jnp.dot(hidden, w_down, preferred_element_type=jnp.float32)  42.3 us
  transfers between devices with their start and end apart: 5, of which 4 were waited for; matrix products, arithmetic and copies ran while one was open for 11% of the time, Pallas kernels for 0%

commit v1 on v0

--- a/solution.py
+++ b/solution.py
@@ -1,13 +1,20 @@
+import functools
 import math
 import jax
 import jax.numpy as jnp
 from jax import lax
+from jax.experimental import pallas as pl
+from jax.experimental.pallas import tpu as pltpu
 from jax.sharding import PartitionSpec as P
 
 HEAD = 128
 WINDOW = 4096
 ROPE_THETA = 50000
 QBLOCK = 256
+CORES = 2
+MESH = pl.DeviceIdType.MESH
+F32 = jnp.float32
+BF16 = jnp.bfloat16
 
 
 def rotary(heads_in, pos_ids):
@@ -52,6 +59,326 @@
     return results.reshape(q_rows, -1)
 
 
+def swap_kernel(wg, wu, wd, wgp, wup, wdp, send_sem, recv_sem):
+    half = wgp.shape[1]
+    tx = lax.axis_index("tx")
+    core = lax.rem(tx, CORES)
+    partner = tx + 1 - 2 * core
+    barrier = pltpu.get_barrier_semaphore()
+    pl.semaphore_signal(barrier, inc=1, device_id={"tx": partner}, device_id_type=MESH)
+    pl.semaphore_wait(barrier, 1)
+    off = pl.multiple_of((1 - core) * half, 128)
+    copies = []
+    for i, (src, dst) in enumerate(((wg.at[:, pl.ds(off, half)], wgp), (wu.at[:, pl.ds(off, half)], wup),
+                                    (wd.at[pl.ds(off, half), :], wdp))):
+        copies.append(pltpu.make_async_remote_copy(src_ref=src, dst_ref=dst, send_sem=send_sem.at[i], recv_sem=recv_sem.at[i],
+                                                   device_id={"tx": partner}, device_id_type=MESH))
+        copies[-1].start()
+    for copy in copies:
+        copy.wait()
+
+
+def swap_weights(wg, wu, wd):
+    half = wg.shape[1] // CORES
+    any_spec = pl.BlockSpec(memory_space=pl.ANY)
+    return pl.pallas_call(
+        swap_kernel,
+        out_shape=(jax.ShapeDtypeStruct((wg.shape[0], half), BF16), jax.ShapeDtypeStruct((wg.shape[0], half), BF16),
+                   jax.ShapeDtypeStruct((half, wd.shape[1]), BF16)),
+        in_specs=[any_spec] * 3, out_specs=[any_spec] * 3,
+        scratch_shapes=[pltpu.SemaphoreType.DMA((3,)), pltpu.SemaphoreType.DMA((3,))],
+        compiler_params=pltpu.CompilerParams(collective_id=0, has_side_effects=True, vmem_limit_bytes=4 << 20),
+    )(wg, wu, wd)
+
+
+SLOTS = 3
+HSLOTS = 8
+
+
+def mlp_kernel(nx, ny, width, n_hbm, base_hbm, wg, wu, wgp, wup, wd, wdp, out_ref,
+               nown, npar, wbuf, w2buf, pbuf, sbuf, rbuf, hid, acc, xrecv, ysend, yrecv,
+               in_sem, w_sem, w2_sem, send_sem, recv_sem, xs_sem, xr_sem, ys_sem, yr_sem, nx_sems, credit, xcredit):
+    tokens, feats = nown.shape
+    bt = tokens // ny
+    ob = bt // nx
+    half = wgp.shape[1]
+    dircols = half // 2
+    chunks = dircols // width
+    total = ny * chunks
+    last_hop = nx - 1
+    kinds = 2 * last_hop
+    tx = lax.axis_index("tx")
+    ty = lax.axis_index("ty")
+    core = lax.rem(tx, CORES)
+    pos = tx // CORES
+    partner = tx + 1 - 2 * core
+
+    def target(d):
+        return lax.rem(pos + 1 + d * (nx - 2), nx) * CORES + core
+
+    def source(d):
+        return lax.rem(pos + nx - 1 - d * (nx - 2), nx) * CORES + core
+
+    def owner_rows(d, step):
+        o = lax.rem(pos + (nx - 1 - step if d == 0 else 1 + step), nx)
+        return pl.ds(pl.multiple_of(o * ob, ob), ob)
+
+    def gather_rows(d, hops):
+        o = lax.rem(pos + (nx - hops if d == 0 else hops), nx)
+        return pl.ds(pl.multiple_of(o * ob, ob), ob)
+
+    def block_rows(p):
+        return pl.ds(pl.multiple_of(lax.rem(ty + 1 + p, ny) * bt, bt), bt)
+
+    barrier = pltpu.get_barrier_semaphore()
+    peers = [{"tx": partner}, {"tx": target(0)}, {"tx": target(1)}] + [{"ty": lax.rem(ty + k, ny)} for k in range(1, ny)]
+    for peer in peers:
+        pl.semaphore_signal(barrier, inc=1, device_id=peer, device_id_type=MESH)
+
+    def w_copies(q, d):
+        slot = lax.rem(q, 2)
+        j = lax.rem(q, chunks)
+        own = pl.ds(pl.multiple_of(core * half + d * dircols + j * width, width), width)
+        par = pl.ds(pl.multiple_of(d * dircols + j * width, width), width)
+        top, low = pl.ds(0, feats), pl.ds(feats, feats)
+        left, right = pl.ds(0, width), pl.ds(width, width)
+        dst = wbuf.at[slot, d]
+        sem = w_sem.at[slot, d]
+        return (pltpu.make_async_copy(wg.at[:, own], dst.at[top, left], sem.at[0]),
+                pltpu.make_async_copy(wu.at[:, own], dst.at[top, right], sem.at[1]),
+                pltpu.make_async_copy(wgp.at[:, par], dst.at[low, left], sem.at[2]),
+                pltpu.make_async_copy(wup.at[:, par], dst.at[low, right], sem.at[3]))
+
+    def w2_copies(q, d):
+        slot = lax.rem(q, 2)
+        j = lax.rem(q, chunks)
+        own = pl.ds(pl.multiple_of(core * half + d * dircols + j * width, width), width)
+        par = pl.ds(pl.multiple_of(d * dircols + j * width, width), width)
+        dst = w2buf.at[slot]
+        rows = pl.ds(d * width, width)
+        sem = w2_sem.at[slot, d]
+        return (pltpu.make_async_copy(wd.at[own, :], dst.at[0, rows, :], sem.at[0]),
+                pltpu.make_async_copy(wdp.at[par, :], dst.at[1, rows, :], sem.at[1]))
+
+    def start(copies):
+        for copy in copies:
+            copy.start()
+
+    def wait(copies):
+        for copy in copies:
+            copy.wait()
+
+    def hop(k, d, t):
+        slot = lax.rem(t, SLOTS)
+        if k < last_hop:
+            src, dst = sbuf.at[d, k, slot], rbuf.at[d, k, slot]
+        else:
+            hslot = lax.rem(t - k + HSLOTS, HSLOTS)
+            rows = gather_rows(d, k - last_hop)
+            src = dst = hid.at[d, hslot, rows, :]
+        return pltpu.make_async_remote_copy(src_ref=src, dst_ref=dst, send_sem=send_sem.at[d, k, slot],
+                                            recv_sem=recv_sem.at[d, k, slot], device_id={"tx": target(d)}, device_id_type=MESH)
+
+    def arrival(k, d, t):
+        slot = lax.rem(t - 1 + SLOTS, SLOTS)
+        if k < last_hop:
+            dst = rbuf.at[d, k, slot]
+        else:
+            hslot = lax.rem(t - 1 - k + HSLOTS, HSLOTS)
+            dst = hid.at[d, hslot, gather_rows(d, k - last_hop + 1), :]
+        pltpu.make_async_remote_copy(src_ref=dst, dst_ref=dst, send_sem=send_sem.at[d, k, slot], recv_sem=recv_sem.at[d, k, slot],
+                                     device_id={"tx": target(d)}, device_id_type=MESH).wait_recv()
+
+    def valid(q):
+        return jnp.logical_and(q >= 0, q < total)
+
+    for d in range(2):
+        start(w_copies(0, d))
+    load_n = pltpu.make_async_copy(n_hbm, nown, in_sem.at[0])
+    load_n.start()
+    pl.semaphore_wait(barrier, len(peers))
+    load_n.wait()
+    swap_n = pltpu.make_async_remote_copy(src_ref=nown, dst_ref=npar, send_sem=nx_sems.at[0], recv_sem=nx_sems.at[1],
+                                          device_id={"tx": partner}, device_id_type=MESH)
+    swap_n.start()
+    swap_n.wait()
+
+    sends = total + kinds - 1
+    signal_end = sends - SLOTS + 1
+
+    def exchange_copy():
+        return pltpu.make_async_remote_copy(src_ref=acc.at[1], dst_ref=xrecv, send_sem=xs_sem, recv_sem=xr_sem,
+                                            device_id={"tx": partner}, device_id_type=MESH)
+
+    def y_copy(p):
+        return pltpu.make_async_remote_copy(src_ref=ysend.at[p], dst_ref=yrecv.at[p], send_sem=ys_sem.at[p], recv_sem=yr_sem.at[p],
+                                            device_id={"ty": lax.rem(ty + 1 + p, ny)}, device_id_type=MESH)
+
+    def tick(t, carry):
+        @pl.when(jnp.logical_and(t >= SLOTS, t < sends))
+        def _():
+            for d in range(2):
+                pl.semaphore_wait(credit.at[d], 1)
+
+        for k in range(kinds):
+            @pl.when(valid(t - SLOTS - k))
+            def _():
+                for d in range(2):
+                    hop(k, d, t - SLOTS).wait_send()
+
+        @pl.when(t < total)
+        def _():
+            for d in range(2):
+                wait(w_copies(t, d))
+
+            @pl.when(t + 1 < total)
+            def _():
+                for d in range(2):
+                    start(w_copies(t + 1, d))
+
+            rows = block_rows(t // chunks)
+            slot = lax.rem(t, 2)
+            pslot = lax.rem(t, nx)
+
+            @pl.loop(0, 2)
+            def _(d):
+                pbuf[d, pslot] = (jnp.dot(nown[rows, :], wbuf[slot, d, :feats, :], preferred_element_type=F32)
+                                  + jnp.dot(npar[rows, :], wbuf[slot, d, feats:, :], preferred_element_type=F32))
+            for d in range(2):
+                sbuf[d, 0, lax.rem(t, SLOTS)] = pbuf[d, pslot, owner_rows(d, 0), :].astype(BF16)
+                hop(0, d, t).start()
+
+        for k in range(1, last_hop + 1):
+            @pl.when(valid(t - k))
+            def _():
+                for d in range(2):
+                    arrival(k - 1, d, t)
+                    part = (pbuf[d, lax.rem(t - k + nx, nx), owner_rows(d, k), :]
+                            + rbuf[d, k - 1, lax.rem(t - 1 + SLOTS, SLOTS)].astype(F32))
+                    if k < last_hop:
+                        sbuf[d, k, lax.rem(t, SLOTS)] = part.astype(BF16)
+                    else:
+                        gate = part[:, :width].astype(BF16).astype(F32)
+                        up = part[:, width:].astype(BF16).astype(F32)
+                        hslot = lax.rem(t - k + HSLOTS, HSLOTS)
+                        hid[d, hslot, gather_rows(d, 0), :] = (gate * jax.nn.sigmoid(gate) * up).astype(BF16)
+                    hop(k, d, t).start()
+
+        for k in range(last_hop + 1, kinds):
+            @pl.when(valid(t - k))
+            def _():
+                for d in range(2):
+                    arrival(k - 1, d, t)
+                    hop(k, d, t).start()
+
+        q = t - kinds
+
+        prev = q - 1
+
+        @pl.when(jnp.logical_and(valid(prev), lax.rem(prev + 1, chunks) == 0))
+        def _():
+            p = prev // chunks
+            copy = exchange_copy()
+            copy.wait()
+
+            @pl.when(p < ny - 1)
+            def _():
+                ysend[p] = (acc[0] + xrecv[...]).astype(BF16)
+                pl.semaphore_signal(xcredit, inc=1, device_id={"tx": partner}, device_id_type=MESH)
+                y_copy(p).start()
+
+            @pl.when(p == ny - 1)
+            def _():
+                out = acc[0] + xrecv[...]
+                for i in range(ny - 1):
+                    y_copy(i).wait_recv()
+                    out += yrecv[i].astype(F32)
+                acc[0] = out
+
+        @pl.when(valid(q))
+        def _():
+            p = q // chunks
+
+            @pl.when(lax.rem(q, chunks) == 0)
+            def _():
+                load = pltpu.make_async_copy(base_hbm.at[block_rows(p), :], acc.at[0], in_sem.at[0])
+                load.start()
+                acc[1] = jnp.zeros_like(acc[1])
+                load.wait()
+
+            for d in range(2):
+                wait(w2_copies(q, d))
+                arrival(kinds - 1, d, t)
+
+            hslot = lax.rem(q, HSLOTS)
+            slot = lax.rem(q, 2)
+
+            @pl.loop(0, 2)
+            def _(o):
+                acc[o] += (jnp.dot(hid[0, hslot], w2buf[slot, o, :width, :], preferred_element_type=F32)
+                           + jnp.dot(hid[1, hslot], w2buf[slot, o, width:, :], preferred_element_type=F32))
+
+            @pl.when(lax.rem(q + 1, chunks) == 0)
+            def _():
+                @pl.when(p > 0)
+                def _():
+                    pl.semaphore_wait(xcredit, 1)
+                exchange_copy().start()
+
+        @pl.when(valid(q + 1))
+        def _():
+            for d in range(2):
+                start(w2_copies(q + 1, d))
+
+        @pl.when(jnp.logical_and(t >= 1, t < signal_end))
+        def _():
+            for d in range(2):
+                pl.semaphore_signal(credit.at[d], inc=1, device_id={"tx": source(d)}, device_id_type=MESH)
+        return carry
+
+    lax.fori_loop(0, total + kinds - 1 + SLOTS, tick, 0)
+    for i in range(ny - 1):
+        y_copy(i).wait_send()
+    store = pltpu.make_async_copy(acc.at[0], out_ref, in_sem.at[0])
+    store.start()
+    store.wait()
+
+
+def mlp_ring(n_all, base, wg, wu, wgp, wup, wd, wdp, nx, ny, width):
+    tokens, feats = n_all.shape
+    bt = tokens // ny
+    ob = bt // nx
+    cols = wd.shape[1]
+    kinds = 2 * (nx - 1)
+    any_spec = pl.BlockSpec(memory_space=pl.ANY)
+    dma = pltpu.SemaphoreType.DMA
+    return pl.pallas_call(
+        functools.partial(mlp_kernel, nx, ny, width),
+        out_shape=jax.ShapeDtypeStruct((bt, cols), F32),
+        in_specs=[any_spec] * 8, out_specs=any_spec,
+        scratch_shapes=[
+            pltpu.VMEM((tokens, feats), BF16),
+            pltpu.VMEM((tokens, feats), BF16),
+            pltpu.VMEM((2, 2, 2 * feats, 2 * width), BF16),
+            pltpu.VMEM((2, 2, 2 * width, cols), BF16),
+            pltpu.VMEM((2, nx, bt, 2 * width), F32),
+            pltpu.VMEM((2, nx - 1, SLOTS, ob, 2 * width), BF16),
+            pltpu.VMEM((2, nx - 1, SLOTS, ob, 2 * width), BF16),
+            pltpu.VMEM((2, HSLOTS, bt, width), BF16),
+            pltpu.VMEM((2, bt, cols), F32),
+            pltpu.VMEM((bt, cols), F32),
+            pltpu.VMEM((ny - 1, bt, cols), BF16),
+            pltpu.VMEM((ny - 1, bt, cols), BF16),
+            dma((1,)), dma((2, 2, 4)), dma((2, 2, 2)),
+            dma((2, kinds, SLOTS)), dma((2, kinds, SLOTS)),
+            dma, dma, dma((ny - 1,)), dma((ny - 1,)), dma((2,)),
+            pltpu.SemaphoreType.REGULAR((2,)), pltpu.SemaphoreType.REGULAR,
+        ],
+        compiler_params=pltpu.CompilerParams(collective_id=1, has_side_effects=True, vmem_limit_bytes=67043328),
+        cost_estimate=pl.CostEstimate(flops=400_000_000_000, bytes_accessed=200_000_000, transcendentals=0),
+    )(n_all, base, wg, wu, wgp, wup, wd, wdp)
+
+
 def solution(mesh):
     tx_size = mesh.shape["tx"]
     ty_size = mesh.shape["ty"]
@@ -59,6 +386,7 @@
     def per_device(x_blk, positions, norm_gain, w_q, w_k, w_v, w_o, w_gate, w_up, w_down):
         d_model = x_blk.shape[1] * tx_size
         seq_len = positions.shape[1]
+        wgp, wup, wdp = swap_weights(w_gate, w_up, w_down)
         x_wide = x_blk.astype(jnp.float32)
         tok_stats = lax.psum(jnp.stack([jnp.sum(x_wide, axis=1), jnp.sum(x_wide * x_wide, axis=1)], axis=1), "tx")
         tok_mean = tok_stats[:, :1] / d_model
@@ -68,15 +396,9 @@
         tokens = n_all.shape[0]
         q_rows = tokens // tx_size
         part_q = jnp.dot(n_all, w_q, preferred_element_type=jnp.float32).astype(jnp.bfloat16)
-        part_rest = tuple(jnp.dot(n_all, w_mat, preferred_element_type=jnp.float32).astype(jnp.bfloat16)
-                          for w_mat in (w_k, w_v, w_gate, w_up))
+        part_rest = tuple(jnp.dot(n_all, w_mat, preferred_element_type=jnp.float32).astype(jnp.bfloat16) for w_mat in (w_k, w_v))
         q_proj = lax.psum_scatter(part_q, "tx", scatter_dimension=0, tiled=True)
-        k_proj, v_proj, gate_act, up_act = lax.psum(part_rest, "tx")
-        if w_k.shape[1] < HEAD:
-            kv_total = w_k.shape[1] * ty_size // HEAD
-            kv_index = lax.axis_index("ty") * kv_total // ty_size
-            k_proj = lax.dynamic_slice_in_dim(lax.all_gather(k_proj, "ty", axis=1, tiled=True), kv_index * HEAD, HEAD, 1)
-            v_proj = lax.dynamic_slice_in_dim(lax.all_gather(v_proj, "ty", axis=1, tiled=True), kv_index * HEAD, HEAD, 1)
+        k_proj, v_proj = lax.psum(part_rest, "tx")
         heads_loc = w_q.shape[1] // HEAD
         kv_loc = k_proj.shape[1] // HEAD
         pos_flat = positions.reshape(tokens)
@@ -87,10 +409,9 @@
         v_heads = v_proj.reshape(tokens, kv_loc, HEAD)
         attn_rows = band_attention(q_rot, k_rot, v_heads, q_first, seq_len)
         attn_all = lax.all_gather(attn_rows, "tx", axis=0, tiled=True)
-        hidden = (jax.nn.silu(gate_act.astype(jnp.float32)) * up_act.astype(jnp.float32)).astype(jnp.bfloat16)
-        block_out = jnp.dot(attn_all, w_o, preferred_element_type=jnp.float32) + jnp.dot(hidden, w_down, preferred_element_type=jnp.float32)
-        block_sum = lax.psum_scatter(block_out.astype(jnp.bfloat16), "ty", scatter_dimension=0, tiled=True)
-        return (x_wide + block_sum.astype(jnp.float32)).astype(jnp.bfloat16)
+        base = jnp.dot(attn_all, w_o, preferred_element_type=jnp.float32)
+        block_sum = mlp_ring(n_all, base, w_gate, w_up, wgp, wup, w_down, wdp, tx_size // CORES, ty_size, 256)
+        return (x_wide + block_sum).astype(jnp.bfloat16)
 
     in_specs = (P(("dp", "ty"), "tx"), P("dp", None), P("tx"), P("tx", "ty"), P("tx", "ty"), P("tx", "ty"),
                 P("ty", "tx"), P("tx", "ty"), P("tx", "ty"), P("ty", "tx"))

time: 868 us -> 628 us (0.72)
  waiting for transfers between devices: 640 us -> 137 us
  Pallas kernels: 0 us -> 362 us
  matrix products: 156 us -> 46.6 us
  local copies, waits for them, and re-layouts: 11.6 us -> 28.9 us
    psum x1, waiting for transfers between devices: 497 us -> 41.2 us  [per_device(): k_proj, v_proj = lax.psum(part_rest, 'tx')]
    pallas_call x0 -> x2, Pallas kernels: none -> 362 us  [the longest x1 330 us: mlp_ring(): pl.pallas_call(functools.partial(mlp_kernel, nx, ny, width), out_shape=ja...]
    dot_general x4 -> x2, matrix products: 75.6 us -> 7.99 us  [per_device(): jnp.dot(n_all, w_mat, preferred_element_type=jnp.float32)]
    all_gather x1, waiting for transfers between devices: 50.9 us -> 2.02 us  [per_device(): attn_all = lax.all_gather(attn_rows, 'tx', axis=0, tiled=True)]
    reduce_scatter x1, waiting for transfers between devices: 0.01 us -> 46.1 us  [per_device(): q_proj = lax.psum_scatter(part_q, 'tx', scatter_dimension=0, tiled=True)]
    reduce_scatter x1 -> x0, waiting for transfers between devices: 44.8 us -> none  [per_device(): lax.psum_scatter(block_out.astype(jnp.bfloat16), 'ty', scatter_dimension=...]
    dot_general x2 -> x1, matrix products: 56.9 us -> 14.6 us  [per_device(): base = jnp.dot(attn_all, w_o, preferred_element_type=jnp.float32)]
    unnamed x15 -> x19, local copies, waits for them, and re-layouts: 1.36 us -> 18.6 us
  transfers between devices with their start and end apart: 5 -> 4, of which waited for: 4 -> 4; matrix products, arithmetic and copies ran while one was open for 11% -> 4% of each run, Pallas kernels for 0% -> 5%
where the time goes in v1:
time: 628 us
  Pallas kernels  362 us (58%)
  waiting for transfers between devices  137 us (22%)
  matrix products  46.6 us (7%)
  local copies, waits for them, and re-layouts  28.9 us (5%)
  other arithmetic  25.4 us (4%)
  blocking collectives  13.9 us (2%)
  between operations  13.4 us (2%)
    pallas_call x1, Pallas kernels, mlp_ring(): pl.pallas_call(functools.partial(mlp_kernel, nx, ny, width), out_shape=ja...  330 us
    all_gather x1, waiting for transfers between devices, per_device(): n_all = lax.all_gather(normed, 'ty', axis=0, tiled=True)  47.8 us
    reduce_scatter x1, waiting for transfers between devices, per_device(): q_proj = lax.psum_scatter(part_q, 'tx', scatter_dimension=0, tiled=True)  46.1 us
    psum x1, waiting for transfers between devices, per_device(): k_proj, v_proj = lax.psum(part_rest, 'tx')  41.2 us
    pallas_call x1, Pallas kernels, swap_weights(): pl.pallas_call(swap_kernel, out_shape=(jax.ShapeDtypeStruct((wg.shape[0],...  31.9 us
    unnamed x19, local copies, waits for them, and re-layouts  18.6 us
    dot_general x1, matrix products, per_device(): base = jnp.dot(attn_all, w_o, preferred_element_type=jnp.float32)  14.6 us
    dot_general x1, matrix products, per_device(): jnp.dot(n_all, w_q, preferred_element_type=jnp.float32).astype(jnp.bfloat16)  14 us
  transfers between devices with their start and end apart: 4, of which 4 were waited for; matrix products, arithmetic and copies ran while one was open for 4% of the time, Pallas kernels for 5%

profile of v1, /device:TPU:97, one launch (start us, length us, event | category | flops | bytes accessed | tf_op | source)
XLA Modules:
  0.0 627.9 jit_solution(6984804359909149968)
XLA Ops:
  6.5 0.0 copy-start.7
  6.5 0.0 all-gather.3.cloned.1.call-start
  6.6 1.7 convert_reduce_fusion
  8.2 13.9 %psum.21 = f32[512,2]{0,1:T(2,128)S(1)} all-reduce(f32[512,2]{0,1:T(2,128)S(1)} %pad_maximum_fusion.2), channel_id=1, replica_groups=mesh['dp'=1,'ty'=4,'tx'=8] {'tx'}, use_global_device_ids=true, to_apply=%region_2.0 | all-reduce | flops 1024 | bytes 8192 | tf_op jit(solution)/shard_map/psum | solution.py:391
  22.1 2.6 fusion.9
  24.7 0.1 all-gather.3.cloned.1.call-update
  24.8 0.1 all-reduce.3.cloned.1.call-start
  24.8 47.8 %all-gather.3.cloned.1.call-done.n_hbm = bf16[2048,1024]{1,0:T(8,128)(2,1)} async-done(((bf16[512,1024]{1,0:T(8,128)(2,1)}), bf16[2048,1024]{1,0:T(8,128)(2,1)}) %all-gather.3.cloned.1.call-update) | async-done | bytes 4194320 | tf_op jit(solution)/shard_map/all_gather | solution.py:395
  72.7 0.0 copy-done.7
  72.7 3.5 convolution_convert_fusion.1
  76.2 0.0 copy-start.8
  76.2 0.7 convert_element_type.63
  76.9 2.0 copy.14
  79.0 0.0 copy-done.8
  79.0 4.5 convolution_convert_fusion.2
  83.5 0.1 all-reduce.3.cloned.1.call-update
  83.5 0.1 reduce-scatter.2.cloned.1.call-start
  83.6 14.0 %convolution_convert_fusion = bf16[2048,2048]{1,0:T(8,128)(2,1)} fusion(bf16[2048,1024]{1,0:T(8,128)(2,1)} %all-gather.3.cloned.1.call-done.n_hbm, bf16[1024,2048]{1,0:T(8,128)(2,1)} %param.13), kind=kOutput, calls=%fused_computation.7 | convolution fusion | flops 8594128896 | bytes 16777216 | tf_op jit(solution)/shard_map/dot_general | solution.py:398
  97.6 0.0 copy-start.5
  97.6 0.1 reduce-scatter.2.cloned.1.call-update
  97.7 0.1 all-gather.5.cloned.1.call-start
  97.8 0.5 copy-done.5
  98.3 0.1 dynamic-slice_convert_fusion
  98.4 0.3 multiply_cosine_fusion.1
  98.7 1.1 fusion.15
  99.8 1.9 multiply_cosine_fusion
  101.7 41.2 %all-reduce.3.cloned.1.call-done = (bf16[2048,2,64,2]{0,1,3,2:T(2,128)(2,1)}, bf16[2048,2,128]{0,2,1:T(8,128)(2,1)}) async-done(((bf16[2048,2,64,2]{0,1,3,2:T(2,128)(2,1)}, bf16[2048,2,128]{0,2,1:T(8,128)(2,1)}), (bf16[2048,2,64,2]{0,1,3,2:T(2,128)(2,1)}, bf16[2048,2,128]{0,2,1:T(8,128)(2,1)})) %all-reduce.3.cloned.1.call-update) | async-done | bytes 2097168 | tf_op jit(solution)/shard_map/psum | solution.py:401
  142.9 2.2 convert_element_type.64
  145.1 1.2 subtract_convert_fusion.1
  146.3 1.4 pad_maximum_fusion
  147.7 1.4 constant_dynamic-slice_fusion
  149.1 1.0 copy.23
  150.1 46.1 %reduce-scatter.2.cloned.1.call-done = bf16[256,2048]{1,0:T(8,128)(2,1)} async-done(((bf16[2048,2048]{1,0:T(8,128)(2,1)}), bf16[256,2048]{1,0:T(8,128)(2,1)}) %reduce-scatter.2.cloned.1.call-update) | async-done | bytes 1048592 | tf_op jit(solution)/shard_map/reduce_scatter | solution.py:400
  196.2 2.6 copy.16
  198.8 2.5 reshape.212
  201.3 2.9 subtract_convert_fusion
  204.2 2.4 pad_maximum_fusion.1
  206.6 1.1 copy.17
  207.7 3.6 fusion.2
  211.3 0.0 copy-start.6
  211.3 4.4 fusion
  215.7 0.0 copy-done.6
  215.7 6.4 %fusion.11 = bf16[256,2,8,128]{0,3,2,1:T(8,128)(2,1)} fusion(f32[2,1280,256,8]{2,1,3,0:T(8,128)S(1)} %get-tuple-element.46, f32[2,8,256]{2,1,0:T(8,128)S(1)} %get-tuple-element.45, pred[256,1280]{0,1:T(8,128)(4,1)S(1)} %fusion.15, f32[256,2,8]{0,2,1:T(8,128)S(1)} %bitcast.57, bf16[2048,2,128]{0,2,1:T(8,128)(2,1)S(1)} %copy-done.6, s32[]{:T(128)S(6)} %min.5), kind=kOutput, calls=%fused_computation.20 | convolution fusion | flops 1364197376 | bytes 23035908 | tf_op jit(solution)/shard_map/while/body/eval_jaxpr/grqk,kgd->qgrd/dot_general | solution.py:55
  222.1 0.1 all-gather.5.cloned.1.call-update
  222.2 0.0 copy-start
  222.2 4.6 copy-done
  226.7 0.0 copy-start.1
  226.7 4.6 copy-done.1
  231.3 31.9 %shard_map.100 = (bf16[1024,3072]{1,0:T(8,128)(2,1)S(1)}, bf16[1024,3072]{1,0:T(8,128)(2,1)S(1)}, bf16[3072,1024]{1,0:T(8,128)(2,1)S(1)}) custom-call(bf16[1024,6144]{1,0:T(8,128)(2,1)S(1)} %copy-done, bf16[1024,6144]{1,0:T(8,128)(2,1)S(1)} %copy-done.1, bf16[6144,1024]{1,0:T(8,128)(2,1)} %wd.3), custom_call_target="tpu_custom_call" | custom-call | tf_op jit(solution)/shard_map/pallas_call | solution.py:84
  263.2 0.0 copy-start.2
  263.3 2.6 copy-done.2
  265.9 0.0 copy-start.3
  265.9 2.6 copy-done.3
  268.5 0.0 copy-start.4
  268.5 2.6 copy-done.4
  271.1 2.0 all-gather.5.cloned.1.call-done
  273.2 14.6 %fusion.29.base_hbm = f32[2048,1024]{1,0:T(8,128)} fusion(bf16[2048,2048]{0,1:T(8,128)(2,1)} %all-gather.5.cloned.1.call-done, bf16[2048,1024]{1,0:T(8,128)(2,1)} %param.16), kind=kOutput, calls=%fused_computation.67 | convolution fusion | flops 8589934592 | bytes 20971520 | tf_op jit(solution)/shard_map/dot_general | solution.py:412
  287.8 330.4 %shard_map.101 = f32[512,1024]{1,0:T(8,128)} custom-call(bf16[2048,1024]{1,0:T(8,128)(2,1)} %all-gather.3.cloned.1.call-done.n_hbm, f32[2048,1024]{1,0:T(8,128)} %fusion.29.base_hbm, bf16[1024,6144]{1,0:T(8,128)(2,1)} %wg.3, bf16[1024,6144]{1,0:T(8,128)(2,1)} %wu.3, bf16[1024,3072]{1,0:T(8,128)(2,1)} %copy-done.2, bf16[1024,3072]{1,0:T(8,128)(2,1)} %copy-done.3, ...), custom_call_target="tpu_custom_call" | custom-call | flops 399999991808 | bytes 200000000 | tf_op jit(solution)/shard_map/pallas_call | solution.py:355
  618.2 3.2 fusion.10
  (6 shorter events, 0.1 us)
Async XLA Ops:
  6.5 66.1 %copy-start.7 = (bf16[1024,256]{1,0:T(8,128)(2,1)S(1)}, bf16[1024,256]{1,0:T(8,128)(2,1)}, u32[]{:S(2)}) copy-start(bf16[1024,256]{1,0:T(8,128)(2,1)} %param.14) | copy-start | bytes 1572868
  6.5 66.1 %all-gather.3.cloned.1.call-start = ((), (), s32[]{:S(2)}) async-start(), calls=%async_computation.1 | async-start | bytes 5242880 | tf_op jit(solution)/shard_map/all_gather | solution.py:395
  24.8 118.1 %all-reduce.3.cloned.1.call-start = ((), (), s32[]{:S(2)}) async-start(), calls=%async_computation.4 | async-start | bytes 4194304 | tf_op jit(solution)/shard_map/psum | solution.py:401
  76.2 2.8 copy-start.8
  83.5 112.7 %reduce-scatter.2.cloned.1.call-start = ((), (), s32[]{:S(2)}) async-start(), calls=%async_computation.2 | async-start | bytes 9437184 | tf_op jit(solution)/shard_map/reduce_scatter | solution.py:400
  97.6 0.7 copy-start.5
  97.7 175.5 %all-gather.5.cloned.1.call-start = ((), (), s32[]{:S(2)}) async-start(), calls=%async_computation.3 | async-start | bytes 9437184 | tf_op jit(solution)/shard_map/all_gather | solution.py:411
  211.3 4.4 copy-start.6
  222.2 4.6 copy-start
  226.7 4.6 copy-start.1
  263.2 2.6 copy-start.2
  265.9 2.6 copy-start.3
  268.5 2.6 copy-start.4
Sparse Core Ops, SparseCore 0:
  24.9 47.7 all-gather.2
  83.6 59.1 all-reduce.2
  145.2 50.9 reduce-scatter.1
  222.3 50.8 all-gather.4

commit v2 on v1

v2 whole, which is shorter than its diff:
```python
import functools
import jax
import jax.numpy as jnp
from jax import lax
from jax.experimental import pallas as pl
from jax.experimental.pallas import tpu as pltpu
from jax.sharding import PartitionSpec as P

HEAD = 128
WINDOW = 4096
ROPE_THETA = 50000
CORES = 2
MESH = pl.DeviceIdType.MESH
F32 = jnp.float32
BF16 = jnp.bfloat16


def swap_lanes(x):
    width = x.shape[1]
    even = lax.rem(lax.broadcasted_iota(jnp.int32, x.shape, 1), 2) == 0
    return jnp.where(even, pltpu.roll(x, width - 1, 1), pltpu.roll(x, 1, 1))


def qkv_kernel(nx, ny, n_hbm, cos_ref, sin_ref, wq, wk, wv, wg, wu, nown_out, npar_out, q_out, kv_out, wgp, wup,
               nown, npar, wbuf, pbuf, sbuf, rbuf, qst, kv, in_sem, w_sem, ws_sem, wr_sem, ns_sem, nr_sem, ps_sem, pr_sem,
               send_sem, recv_sem, ks_sem, kr_sem, gs_sem, gr_sem):
    tokens, feats = nown.shape
    bt = tokens // ny
    hb = bt // 2
    ob = bt // nx
    half = wgp.shape[1]
    qcols = wq.shape[1] // CORES // 2
    hops = nx - 1
    order = (0, 1, 3, 2)
    tx = lax.axis_index("tx")
    ty = lax.axis_index("ty")
    core = lax.rem(tx, CORES)
    pos = tx // CORES
    partner = tx + 1 - 2 * core
    north, south = lax.rem(ty + 1, ny), lax.rem(ty + ny - 1, ny)

    def chip(i):
        return lax.rem(pos + i, nx) * CORES + core

    def owner_rows(d, step):
        o = lax.rem(pos + (nx - 1 - step if d == 0 else 1 + step), nx)
        return pl.ds(pl.multiple_of(o * ob, ob), ob)

    def rows_of(off):
        return pl.ds(pl.multiple_of(lax.rem(ty + off, ny) * bt, bt), bt)

    def half_rows(off, i):
        return pl.ds(pl.multiple_of(lax.rem(ty + off, ny) * bt + i * hb, hb), hb)

    def remote(src, dst, send, recv, device):
        return pltpu.make_async_remote_copy(src_ref=src, dst_ref=dst, send_sem=send, recv_sem=recv, device_id=device, device_id_type=MESH)

    barrier = pltpu.get_barrier_semaphore()
    peers = [{"tx": partner}] + [{"tx": chip(i)} for i in range(1, nx)] + [{"ty": lax.rem(ty + k, ny)} for k in range(1, ny)]
    for peer in peers:
        pl.semaphore_signal(barrier, inc=1, device_id=peer, device_id_type=MESH)

    load_n = pltpu.make_async_copy(n_hbm, nown.at[rows_of(0), :], in_sem.at[0])
    load_n.start()

    def w_parts(c):
        parts = []
        for d in range(2):
            col = pl.ds(pl.multiple_of(c * 2 * qcols + d * qcols, 128), qcols)
            small = pl.ds(pl.multiple_of(c * HEAD, HEAD), HEAD)
            parts.append((wq.at[:, col], d, pl.ds(0, qcols)))
            parts.append(((wk if d == 0 else wv).at[:, small], d, pl.ds(qcols, HEAD)))
        return parts

    local_w = [pltpu.make_async_copy(s, wbuf.at[d, pl.ds(0, feats), cols], w_sem.at[i]) for i, (s, d, cols) in enumerate(w_parts(core))]
    for copy in local_w:
        copy.start()
    pl.semaphore_wait(barrier, len(peers))
    load_n.wait()

    own = nown.at[rows_of(0), :]
    swap_w = [remote(s, wbuf.at[d, pl.ds(feats, feats), cols], ws_sem.at[i], wr_sem.at[i], {"tx": partner})
              for i, (s, d, cols) in enumerate(w_parts(1 - core))]
    to_south = remote(own, own, ns_sem.at[0], nr_sem.at[0], {"ty": south})
    to_north = remote(own, own, ns_sem.at[1], nr_sem.at[1], {"ty": north})
    to_south.start()
    to_north.start()

    def pair(p):
        rows = rows_of(order[p])
        return remote(nown.at[rows, :], npar.at[rows, :], ps_sem.at[p], pr_sem.at[p], {"tx": partner})

    def far(i):
        rows = half_rows(1 if i == 0 else ny - 1, i)
        return remote(nown.at[rows, :], nown.at[rows, :], ns_sem.at[2 + i], nr_sem.at[2 + i], {"ty": south if i == 0 else north})

    def far_arrival(i):
        rows = half_rows(2, i)
        return remote(nown.at[rows, :], nown.at[rows, :], ns_sem.at[2 + i], nr_sem.at[2 + i], {"ty": south if i == 0 else north})

    def near_arrival(i):
        rows = rows_of(1 if i == 0 else ny - 1)
        return remote(nown.at[rows, :], nown.at[rows, :], ns_sem.at[i], nr_sem.at[i], {"ty": south if i == 0 else north})

    pair(0).start()
    for copy in swap_w:
        copy.start()

    piece = feats // ny
    goff = pl.multiple_of((1 - core) * half, 128)

    def swap_mlp(i):
        rows = pl.ds(i * piece, piece)
        return [remote(src.at[rows, pl.ds(goff, half)], dst.at[rows, :], gs_sem.at[k, i], gr_sem.at[k, i], {"tx": partner})
                for k, (src, dst) in enumerate(((wg, wgp), (wu, wup)))]

    def hop(k, d, p):
        target = chip(1 if d == 0 else nx - 1)
        return remote(sbuf.at[d, k, p], rbuf.at[d, k, p], send_sem.at[d, k, p], recv_sem.at[d, k, p], {"tx": target})

    def kv_rows(p):
        return pl.ds(pl.multiple_of(lax.rem(ty + order[p], ny) * bt + pos * ob, ob), ob)

    def kv_copy(d, p, i):
        rows = kv_rows(p)
        return remote(kv.at[d, rows, :], kv.at[d, rows, :], ks_sem.at[d, p, i - 1], kr_sem.at[d, p, i - 1], {"tx": chip(i)})

    def kv_arrival(d, p, i):
        rows = pl.ds(pl.multiple_of(lax.rem(ty + order[p], ny) * bt + lax.rem(pos + nx - i, nx) * ob, ob), ob)
        return remote(kv.at[d, rows, :], kv.at[d, rows, :], ks_sem.at[d, p, i - 1], kr_sem.at[d, p, i - 1], {"tx": chip(i)})

    def n_store(p):
        rows = rows_of(order[p])
        return (pltpu.make_async_copy(nown.at[rows, :], nown_out.at[rows, :], in_sem.at[1 + 2 * p]),
                pltpu.make_async_copy(npar.at[rows, :], npar_out.at[rows, :], in_sem.at[2 + 2 * p]))

    for t in range(ny + hops):
        if t < ny:
            if t == 1:
                near_arrival(0).wait_recv()
                far(0).start()
                pair(1).start()
                near_arrival(1).wait_recv()
                far(1).start()
                pair(2).start()
            if t == 3:
                far_arrival(0).wait_recv()
                far_arrival(1).wait_recv()
                pair(3).start()
            pair(t).wait_recv()
            for copy in n_store(t):
                copy.start()
            if t == 0:
                for copy in local_w:
                    copy.wait()
                for copy in swap_w:
                    copy.wait_recv()
            rows = rows_of(order[t])

            @pl.loop(0, 2)
            def _(d):
                pbuf[d, t % nx] = (jnp.dot(nown[rows, :], wbuf[d, :feats, :], preferred_element_type=F32)
                                   + jnp.dot(npar[rows, :], wbuf[d, feats:, :], preferred_element_type=F32))
            for d in range(2):
                sbuf[d, 0, t] = pbuf[d, t % nx, owner_rows(d, 0), :].astype(BF16)
                hop(0, d, t).start()
            for copy in swap_mlp(t):
                copy.start()
        for k in range(1, hops + 1):
            p = t - k
            if 0 <= p < ny:
                for d in range(2):
                    hop(k - 1, d, p).wait_recv()
                    part = pbuf[d, p % nx, owner_rows(d, k), :] + rbuf[d, k - 1, p].astype(F32)
                    if k < hops:
                        sbuf[d, k, p] = part.astype(BF16)
                        hop(k, d, p).start()
                        continue
                    rows = kv_rows(p)
                    block = lax.rem(ty + order[p], ny)
                    part = part.astype(BF16).astype(F32)
                    cos, sin = cos_ref[rows, :], sin_ref[rows, :]
                    small = part[:, qcols:]
                    if d == 0:
                        small = small * cos + swap_lanes(small) * sin
                    kv[d, rows, :] = small.astype(BF16)
                    for i in range(1, nx):
                        kv_copy(d, p, i).start()
                    for h in range(qcols // HEAD):
                        head = part[:, h * HEAD:(h + 1) * HEAD]
                        qst[block, :, d * qcols + h * HEAD:d * qcols + (h + 1) * HEAD] = (head * cos + swap_lanes(head) * sin).astype(BF16)

    for p in range(ny):
        for d in range(2):
            for i in range(1, nx):
                kv_arrival(d, p, i).wait_recv()
                kv_copy(d, p, i).wait_send()
            for k in range(hops):
                hop(k, d, p).wait_send()
        pair(p).wait_send()
        for copy in n_store(p):
            copy.wait()
        for copy in swap_mlp(p):
            copy.wait()
    for copy in swap_w:
        copy.wait_send()
    to_south.wait_send()
    to_north.wait_send()
    far(0).wait_send()
    far(1).wait_send()
    stores = (pltpu.make_async_copy(qst, q_out, in_sem.at[0]), pltpu.make_async_copy(kv, kv_out, in_sem.at[1]))
    for copy in stores:
        copy.start()
    for copy in stores:
        copy.wait()


def qkv_ring(n_blk, cos, sin, wq, wk, wv, wg, wu, nx, ny):
    bt, feats = n_blk.shape
    tokens = bt * ny
    ob = bt // nx
    half = wg.shape[1] // CORES
    qhalf = wq.shape[1] // CORES
    cols = qhalf // 2 + HEAD
    hops = nx - 1
    any_spec = pl.BlockSpec(memory_space=pl.ANY)
    vmem = pl.BlockSpec(memory_space=pltpu.VMEM)
    dma = pltpu.SemaphoreType.DMA
    sds = jax.ShapeDtypeStruct
    return pl.pallas_call(
        functools.partial(qkv_kernel, nx, ny),
        out_shape=(sds((tokens, feats), BF16), sds((tokens, feats), BF16), sds((ny, ob, qhalf), BF16), sds((2, tokens, HEAD), BF16),
                   sds((feats, half), BF16), sds((feats, half), BF16)),
        in_specs=[any_spec, vmem, vmem] + [any_spec] * 5, out_specs=[any_spec] * 6,
        scratch_shapes=[
            pltpu.VMEM((tokens, feats), BF16), pltpu.VMEM((tokens, feats), BF16),
            pltpu.VMEM((2, 2 * feats, cols), BF16),
            pltpu.VMEM((2, nx, bt, cols), F32),
            pltpu.VMEM((2, hops, ny, ob, cols), BF16), pltpu.VMEM((2, hops, ny, ob, cols), BF16),
            pltpu.VMEM((ny, ob, qhalf), BF16), pltpu.VMEM((2, tokens, HEAD), BF16),
            dma((1 + 2 * ny,)), dma((4,)), dma((4,)), dma((4,)), dma((4,)), dma((4,)), dma((ny,)), dma((ny,)),
            dma((2, hops, ny)), dma((2, hops, ny)), dma((2, ny, hops)), dma((2, ny, hops)), dma((2, ny)), dma((2, ny)),
        ],
        compiler_params=pltpu.CompilerParams(collective_id=0, has_side_effects=True, vmem_limit_bytes=60 << 20),
        cost_estimate=pl.CostEstimate(flops=60_000_000_000, bytes_accessed=60_000_000, transcendentals=0),
    )(n_blk, cos, sin, wq, wk, wv, wg, wu)


SLOTS = 3
HSLOTS = 8


def mlp_kernel(nx, ny, width, seq_len, nown_hbm, npar_hbm, q_hbm, kv_hbm, wg, wu, wgp, wup, wd, wo, out_ref, wdp, wop,
               nown, npar, wbuf, w2buf, pbuf, sbuf, rbuf, hid, acc, xrecv, ysend, yrecv, qst, kv, abuf,
               in_sem, n_sem, w_sem, w2_sem, send_sem, recv_sem, xs_sem, xr_sem, ys_sem, yr_sem, gs_sem, gr_sem, credit, xcredit):
    tokens, feats = nown.shape
    bt = tokens // ny
    ob = bt // nx
    half = wgp.shape[1]
    dircols = half // 2
    ahalf = wop.shape[0]
    adir = ahalf // 2
    mlp_chunks = dircols // width
    chunks = mlp_chunks + adir // width
    total = ny * chunks
    last_hop = nx - 1
    kinds = 2 * last_hop
    tx = lax.axis_index("tx")
    ty = lax.axis_index("ty")
    core = lax.rem(tx, CORES)
    pos = tx // CORES
    partner = tx + 1 - 2 * core

    def target(d):
        return lax.rem(pos + 1 + d * (nx - 2), nx) * CORES + core

    def source(d):
        return lax.rem(pos + nx - 1 - d * (nx - 2), nx) * CORES + core

    def owner_rows(d, step):
        o = lax.rem(pos + (nx - 1 - step if d == 0 else 1 + step), nx)
        return pl.ds(pl.multiple_of(o * ob, ob), ob)

    def gather_rows(d, hops):
        o = lax.rem(pos + (nx - hops if d == 0 else hops), nx)
        return pl.ds(pl.multiple_of(o * ob, ob), ob)

    def block_rows(p):
        return pl.ds(pl.multiple_of(lax.rem(ty + 1 + p, ny) * bt, bt), bt)

    barrier = pltpu.get_barrier_semaphore()
    peers = [{"tx": partner}, {"tx": target(0)}, {"tx": target(1)}] + [{"ty": lax.rem(ty + k, ny)} for k in range(1, ny)]
    for peer in peers:
        pl.semaphore_signal(barrier, inc=1, device_id=peer, device_id_type=MESH)

    def w_copies(q, d):
        slot = lax.rem(q, 2)
        j = lax.rem(q, chunks)
        own = pl.ds(pl.multiple_of(core * half + d * dircols + j * width, width), width)
        par = pl.ds(pl.multiple_of(d * dircols + j * width, width), width)
        top, low = pl.ds(0, feats), pl.ds(feats, feats)
        left, right = pl.ds(0, width), pl.ds(width, width)
        dst = wbuf.at[slot, d]
        sem = w_sem.at[slot, d]
        return (pltpu.make_async_copy(wg.at[:, own], dst.at[top, left], sem.at[0]),
                pltpu.make_async_copy(wu.at[:, own], dst.at[top, right], sem.at[1]),
                pltpu.make_async_copy(wgp.at[:, par], dst.at[low, left], sem.at[2]),
                pltpu.make_async_copy(wup.at[:, par], dst.at[low, right], sem.at[3]))

    def w2_copies(q, d, mlp):
        slot = lax.rem(q, 2)
        j = lax.rem(q, chunks)
        dst = w2buf.at[slot]
        rows = pl.ds(d * width, width)
        sem = w2_sem.at[slot, d]
        if mlp:
            mine, theirs, size, first = wd, wdp, half, d * dircols + j * width
        else:
            mine, theirs, size, first = wo, wop, ahalf, d * adir + (j - mlp_chunks) * width
        own = pl.ds(pl.multiple_of(core * size + first, width), width)
        par = pl.ds(pl.multiple_of(first, width), width)
        return (pltpu.make_async_copy(mine.at[own, :], dst.at[0, rows, :], sem.at[0]),
                pltpu.make_async_copy(theirs.at[par, :], dst.at[1, rows, :], sem.at[1]))

    def w2_each(q, action):
        @pl.when(is_mlp(q))
        def _():
            for d in range(2):
                action(w2_copies(q, d, True))

        @pl.when(jnp.logical_not(is_mlp(q)))
        def _():
            for d in range(2):
                action(w2_copies(q, d, False))

    def start(copies):
        for copy in copies:
            copy.start()

    def wait(copies):
        for copy in copies:
            copy.wait()

    def hop(k, d, t):
        slot = lax.rem(t, SLOTS)
        if k < last_hop:
            src, dst = sbuf.at[d, k, slot], rbuf.at[d, k, slot]
        else:
            hslot = lax.rem(t - k + HSLOTS, HSLOTS)
            rows = gather_rows(d, k - last_hop)
            src = dst = hid.at[d, hslot, rows, :]
        return pltpu.make_async_remote_copy(src_ref=src, dst_ref=dst, send_sem=send_sem.at[d, k, slot],
                                            recv_sem=recv_sem.at[d, k, slot], device_id={"tx": target(d)}, device_id_type=MESH)

    def arrival(k, d, t):
        slot = lax.rem(t - 1 + SLOTS, SLOTS)
        if k < last_hop:
            dst = rbuf.at[d, k, slot]
        else:
            hslot = lax.rem(t - 1 - k + HSLOTS, HSLOTS)
            dst = hid.at[d, hslot, gather_rows(d, k - last_hop + 1), :]
        pltpu.make_async_remote_copy(src_ref=dst, dst_ref=dst, send_sem=send_sem.at[d, k, slot], recv_sem=recv_sem.at[d, k, slot],
                                     device_id={"tx": target(d)}, device_id_type=MESH).wait_recv()

    def valid(q):
        return jnp.logical_and(q >= 0, q < total)

    def is_mlp(q):
        return lax.rem(q, chunks) < mlp_chunks

    def reduces(q):
        return jnp.logical_and(valid(q), is_mlp(q))

    def n_copies(p):
        rows = block_rows(p)
        return (pltpu.make_async_copy(nown_hbm.at[rows, :], nown.at[rows, :], n_sem.at[0, p]),
                pltpu.make_async_copy(npar_hbm.at[rows, :], npar.at[rows, :], n_sem.at[1, p]))

    start(n_copies(0))
    for d in range(2):
        start(w_copies(0, d))
    for p in range(1, ny):
        start(n_copies(p))
    loads = (pltpu.make_async_copy(q_hbm, qst, in_sem.at[0]), pltpu.make_async_copy(kv_hbm, kv, in_sem.at[1]))
    start(loads)
    pl.semaphore_wait(barrier, len(peers))
    swaps = []
    for i, (src, dst, size) in enumerate(((wd, wdp, half), (wo, wop, ahalf))):
        rows = pl.ds(pl.multiple_of((1 - core) * size, width), size)
        swaps.append(pltpu.make_async_remote_copy(src_ref=src.at[rows, :], dst_ref=dst, send_sem=gs_sem.at[i], recv_sem=gr_sem.at[i],
                                                  device_id={"tx": partner}, device_id_type=MESH))
    start(swaps)
    wait(loads)

    def attention(p):
        block = lax.rem(ty + 1 + p, ny)
        first = block * bt
        key0 = pl.multiple_of(first // seq_len * seq_len, seq_len)
        keys = kv[0, pl.ds(key0, seq_len), :]
        vals = kv[1, pl.ds(key0, seq_len), :]
        group = 4
        shape = (group * ob, seq_len)
        gap = (first + pos * ob + lax.rem(lax.broadcasted_iota(jnp.int32, shape, 0), ob)
               - key0 - lax.broadcasted_iota(jnp.int32, shape, 1))
        allowed = jnp.logical_and(gap >= 0, gap < WINDOW)
        for g in range(ahalf // HEAD // group):
            cols = [slice((g * group + h) * HEAD, (g * group + h + 1) * HEAD) for h in range(group)]
            queries = jnp.concatenate([qst[block, :, c] for c in cols], axis=0)
            scores = lax.dot_general(queries, keys, (((1,), (1,)), ((), ())), preferred_element_type=F32) * HEAD ** -0.5
            scores = jnp.where(allowed, scores, -1e30)
            weights = jnp.exp(scores - jnp.max(scores, axis=1, keepdims=True))
            norm = jnp.sum(weights, axis=1, keepdims=True)
            mixed = jnp.dot(weights.astype(BF16), vals, preferred_element_type=F32) / norm
            for h, c in enumerate(cols):
                abuf[:, c] = mixed[h * ob:(h + 1) * ob].astype(BF16)

    sends = total + kinds - 1
    signal_end = sends - SLOTS + 1

    def exchange_copy():
        return pltpu.make_async_remote_copy(src_ref=acc.at[1], dst_ref=xrecv, send_sem=xs_sem, recv_sem=xr_sem,
                                            device_id={"tx": partner}, device_id_type=MESH)

    def y_copy(p):
        return pltpu.make_async_remote_copy(src_ref=ysend.at[p], dst_ref=yrecv.at[p], send_sem=ys_sem.at[p], recv_sem=yr_sem.at[p],
                                            device_id={"ty": lax.rem(ty + 1 + p, ny)}, device_id_type=MESH)

    def tick(t, carry):
        @pl.when(jnp.logical_and(t >= SLOTS, t < sends))
        def _():
            for d in range(2):
                pl.semaphore_wait(credit.at[d], 1)

        for k in range(kinds):
            @pl.when((reduces if k < last_hop else valid)(t - SLOTS - k))
            def _():
                for d in range(2):
                    hop(k, d, t - SLOTS).wait_send()

        @pl.when(reduces(t + 1))
        def _():
            for d in range(2):
                start(w_copies(t + 1, d))

        @pl.when(reduces(t))
        def _():
            for d in range(2):
                wait(w_copies(t, d))

            @pl.when(lax.rem(t, chunks) == 0)
            def _():
                wait(n_copies(t // chunks))

            rows = block_rows(t // chunks)
            slot = lax.rem(t, 2)
            pslot = lax.rem(t, nx)

            @pl.loop(0, 2)
            def _(d):
                pbuf[d, pslot] = (jnp.dot(nown[rows, :], wbuf[slot, d, :feats, :], preferred_element_type=F32)
                                  + jnp.dot(npar[rows, :], wbuf[slot, d, feats:, :], preferred_element_type=F32))
            for d in range(2):
                sbuf[d, 0, lax.rem(t, SLOTS)] = pbuf[d, pslot, owner_rows(d, 0), :].astype(BF16)
                hop(0, d, t).start()

        for k in range(1, last_hop + 1):
            @pl.when(reduces(t - k))
            def _():
                for d in range(2):
                    arrival(k - 1, d, t)
                    part = (pbuf[d, lax.rem(t - k + nx, nx), owner_rows(d, k), :]
                            + rbuf[d, k - 1, lax.rem(t - 1 + SLOTS, SLOTS)].astype(F32))
                    if k < last_hop:
                        sbuf[d, k, lax.rem(t, SLOTS)] = part.astype(BF16)
                    else:
                        gate = part[:, :width].astype(BF16).astype(F32)
                        up = part[:, width:].astype(BF16).astype(F32)
                        hslot = lax.rem(t - k + HSLOTS, HSLOTS)
                        hid[d, hslot, gather_rows(d, 0), :] = (gate * jax.nn.sigmoid(gate) * up).astype(BF16)
                    hop(k, d, t).start()

        for i in range(adir // width):
            q = t - last_hop

            @pl.when(jnp.logical_and(valid(q), lax.rem(q, chunks) == mlp_chunks + i))
            def _():
                for d in range(2):
                    hslot = lax.rem(q + HSLOTS, HSLOTS)
                    hid[d, hslot, gather_rows(d, 0), :] = abuf[:, d * adir + i * width:d * adir + (i + 1) * width]
                    hop(last_hop, d, t).start()

        for k in range(last_hop + 1, kinds):
            @pl.when(valid(t - k))
            def _():
                for d in range(2):
                    arrival(k - 1, d, t)
                    hop(k, d, t).start()

        q = t - kinds

        prev = q - 1

        @pl.when(jnp.logical_and(valid(prev), lax.rem(prev + 1, chunks) == 0))
        def _():
            p = prev // chunks
            copy = exchange_copy()
            copy.wait()

            @pl.when(p < ny - 1)
            def _():
                ysend[p] = (acc[0] + xrecv[...]).astype(BF16)
                pl.semaphore_signal(xcredit, inc=1, device_id={"tx": partner}, device_id_type=MESH)
                y_copy(p).start()

            @pl.when(p == ny - 1)
            def _():
                out = acc[0] + xrecv[...]
                for i in range(ny - 1):
                    y_copy(i).wait_recv()
                    out += yrecv[i].astype(F32)
                acc[0] = out

        @pl.when(valid(q))
        def _():
            p = q // chunks

            @pl.when(lax.rem(q, chunks) == 0)
            def _():
                acc[...] = jnp.zeros_like(acc)

            w2_each(q, wait)
            for d in range(2):
                arrival(kinds - 1, d, t)

            hslot = lax.rem(q, HSLOTS)
            slot = lax.rem(q, 2)

            @pl.loop(0, 2)
            def _(o):
                acc[o] += (jnp.dot(hid[0, hslot], w2buf[slot, o, :width, :], preferred_element_type=F32)
                           + jnp.dot(hid[1, hslot], w2buf[slot, o, width:, :], preferred_element_type=F32))

            @pl.when(lax.rem(q + 1, chunks) == 0)
            def _():
                @pl.when(p > 0)
                def _():
                    pl.semaphore_wait(xcredit, 1)
                exchange_copy().start()

        @pl.when(q + 1 == 0)
        def _():
            for copy in swaps:
                copy.wait_recv()

        @pl.when(valid(q + 1))
        def _():
            w2_each(q + 1, start)

        @pl.when(jnp.logical_and(t < total, lax.rem(t, chunks) == chunks // 2))
        def _():
            attention(t // chunks)

        @pl.when(jnp.logical_and(t >= 1, t < signal_end))
        def _():
            for d in range(2):
                pl.semaphore_signal(credit.at[d], inc=1, device_id={"tx": source(d)}, device_id_type=MESH)
        return carry

    lax.fori_loop(0, total + kinds - 1 + SLOTS, tick, 0)
    for i in range(ny - 1):
        y_copy(i).wait_send()
    for copy in swaps:
        copy.wait_send()
    store = pltpu.make_async_copy(acc.at[0], out_ref, in_sem.at[0])
    store.start()
    store.wait()


def mlp_ring(n_own, n_par, q, kv, wg, wu, wgp, wup, wd, wo, nx, ny, width, seq_len):
    tokens, feats = n_own.shape
    bt = tokens // ny
    ob = bt // nx
    cols = wd.shape[1]
    half = wgp.shape[1]
    ahalf = wo.shape[0] // CORES
    kinds = 2 * (nx - 1)
    any_spec = pl.BlockSpec(memory_space=pl.ANY)
    dma = pltpu.SemaphoreType.DMA
    sds = jax.ShapeDtypeStruct
    return pl.pallas_call(
        functools.partial(mlp_kernel, nx, ny, width, seq_len),
        out_shape=(sds((bt, cols), F32), sds((half, cols), BF16), sds((ahalf, cols), BF16)),
        in_specs=[any_spec] * 10, out_specs=[any_spec] * 3,
        scratch_shapes=[
            pltpu.VMEM((tokens, feats), BF16),
            pltpu.VMEM((tokens, feats), BF16),
            pltpu.VMEM((2, 2, 2 * feats, 2 * width), BF16),
            pltpu.VMEM((2, 2, 2 * width, cols), BF16),
            pltpu.VMEM((2, nx, bt, 2 * width), F32),
            pltpu.VMEM((2, nx - 1, SLOTS, ob, 2 * width), BF16),
            pltpu.VMEM((2, nx - 1, SLOTS, ob, 2 * width), BF16),
            pltpu.VMEM((2, HSLOTS, bt, width), BF16),
            pltpu.VMEM((2, bt, cols), F32),
            pltpu.VMEM((bt, cols), F32),
            pltpu.VMEM((ny - 1, bt, cols), BF16),
            pltpu.VMEM((ny - 1, bt, cols), BF16),
            pltpu.VMEM(q.shape, BF16), pltpu.VMEM(kv.shape, BF16), pltpu.VMEM((ob, ahalf), BF16),
            dma((2,)), dma((2, ny)), dma((2, 2, 4)), dma((2, 2, 2)),
            dma((2, kinds, SLOTS)), dma((2, kinds, SLOTS)),
            dma, dma, dma((ny - 1,)), dma((ny - 1,)), dma((2,)), dma((2,)),
            pltpu.SemaphoreType.REGULAR((2,)), pltpu.SemaphoreType.REGULAR,
        ],
        compiler_params=pltpu.CompilerParams(collective_id=1, has_side_effects=True, vmem_limit_bytes=67043328),
        cost_estimate=pl.CostEstimate(flops=400_000_000_000, bytes_accessed=200_000_000, transcendentals=0),
    )(n_own, n_par, q, kv, wg, wu, wgp, wup, wd, wo)


def solution(mesh):
    tx_size = mesh.shape["tx"]
    ty_size = mesh.shape["ty"]
    nx = tx_size // CORES

    def per_device(x_blk, positions, norm_gain, w_q, w_k, w_v, w_o, w_gate, w_up, w_down):
        d_model = x_blk.shape[1] * tx_size
        seq_len = positions.shape[1]
        inv_freq = ROPE_THETA ** (-2.0 * (jnp.arange(HEAD) // 2).astype(F32) / HEAD)
        angle = positions.reshape(-1).astype(F32)[:, None] * inv_freq[None, :]
        cos = jnp.cos(angle)
        sin = jnp.sin(angle) * jnp.where(jnp.arange(HEAD) % 2 == 0, -1.0, 1.0).astype(F32)
        x_wide = x_blk.astype(F32)
        tok_stats = lax.psum(jnp.stack([jnp.sum(x_wide, axis=1), jnp.sum(x_wide * x_wide, axis=1)], axis=1), "tx")
        tok_mean = tok_stats[:, :1] / d_model
        tok_var = tok_stats[:, 1:] / d_model - tok_mean * tok_mean
        normed = (norm_gain * (x_wide - tok_mean) * lax.rsqrt(tok_var + 1e-5)).astype(BF16)
        n_own, n_par, q, kv, wgp, wup = qkv_ring(normed, cos, sin, w_q, w_k, w_v, w_gate, w_up, nx, ty_size)
        block_sum, _, _ = mlp_ring(n_own, n_par, q, kv, w_gate, w_up, wgp, wup, w_down, w_o, nx, ty_size, 256, seq_len)
        return (x_wide + block_sum).astype(BF16)

    in_specs = (P(("dp", "ty"), "tx"), P("dp", None), P("tx"), P("tx", "ty"), P("tx", "ty"), P("tx", "ty"),
                P("ty", "tx"), P("tx", "ty"), P("tx", "ty"), P("ty", "tx"))
    return jax.shard_map(per_device, mesh=mesh, in_specs=in_specs, out_specs=P(("dp", "ty"), "tx"), check_vma=False)
```

time: 628 us -> 479 us (0.76)
  waiting for transfers between devices: 137 us -> 0 us
  Pallas kernels: 362 us -> 451 us
  matrix products: 46.6 us -> 0 us
  local copies, waits for them, and re-layouts: 28.9 us -> 0.01 us
  between operations: 13.4 us -> 0.03 us
  other arithmetic: 25.4 us -> 13.7 us
    pallas_call x2, Pallas kernels: 362 us -> 451 us  [the longest x1 360 us: mlp_ring(): pl.pallas_call(functools.partial(mlp_kernel, nx, ny, width, seq_len), out...]
    all_gather x2 -> x0, waiting for transfers between devices: 49.9 us -> none  [the longest x1 47.8 us: per_device(): n_all = lax.all_gather(normed, 'ty', axis=0, tiled=True)]
    dot_general x6 -> x0, matrix products: 46.6 us -> none  [the longest x1 14.6 us: per_device(): base = jnp.dot(attn_all, w_o, preferred_element_type=jnp.float32)]
    reduce_scatter x1 -> x0, waiting for transfers between devices: 46.1 us -> none  [per_device(): q_proj = lax.psum_scatter(part_q, 'tx', scatter_dimension=0, tiled=True)]
    psum x1 -> x0, waiting for transfers between devices: 41.2 us -> none  [per_device(): k_proj, v_proj = lax.psum(part_rest, 'tx')]
    unnamed x19 -> x1, local copies, waits for them, and re-layouts: 18.6 us -> 0.01 us
    another operation x4 -> x0, other arithmetic: 7.91 us -> none
    convert_element_type x4 -> x0, local copies, waits for them, and re-layouts: 7.83 us -> none  [rotary(): heads_in.astype(jnp.float32).reshape(heads_in.shape[:-1] + (half_dim, 2))]
  transfers between devices with their start and end apart: 4 -> 0, of which waited for: 4 -> 0; matrix products, arithmetic and copies ran while one was open for 4% -> 0% of each run, Pallas kernels for 5% -> 0%
where the time goes in v2:
time: 479 us
  Pallas kernels  451 us (94%)
  blocking collectives  13.9 us (3%)
  other arithmetic  13.7 us (3%)
    pallas_call x1, Pallas kernels, mlp_ring(): pl.pallas_call(functools.partial(mlp_kernel, nx, ny, width, seq_len), out...  360 us
    pallas_call x1, Pallas kernels, qkv_ring(): pl.pallas_call(functools.partial(qkv_kernel, nx, ny), out_shape=(sds((tok...  90.7 us
    psum x1, blocking collectives, per_device(): lax.psum(jnp.stack([jnp.sum(x_wide, axis=1), jnp.sum(x_wide * x_wide, axi...  13.9 us

profile of v2, /device:TPU:97, one launch (start us, length us, event | category | flops | bytes accessed | tf_op | source)
XLA Modules:
  0.0 478.6 jit_solution(11874380109341894557)
XLA Ops:
  0.0 1.6 convert_reduce_fusion
  1.7 13.9 %psum.7 = f32[512,2]{0,1:T(2,128)S(1)} all-reduce(f32[512,2]{0,1:T(2,128)S(1)} %pad_maximum_fusion), channel_id=1, replica_groups=mesh['dp'=1,'ty'=4,'tx'=8] {'tx'}, use_global_device_ids=true, to_apply=%region_2.3 | all-reduce | flops 1024 | bytes 8192 | tf_op jit(solution)/shard_map/psum | solution.py:631
  15.5 0.7 convert_bitcast_fusion
  16.2 2.6 fusion.3.n_hbm
  18.8 5.6 %fusion.5 = (f32[2048,128]{1,0:T(8,128)}, f32[2048,128]{1,0:T(8,128)}) fusion(f32[128]{0:T(128)S(1)} %get-tuple-element.25, f32[128]{0:T(128)S(1)} %get-tuple-element.26, f32[2048]{0:T(1024)S(1)} %bitcast.9), kind=kLoop, calls=%fused_computation.11 | loop fusion | flops 524288 | bytes 2106368 | tf_op jit(solution)/shard_map/mul | solution.py:629
  24.4 90.7 %shard_map.100 = (bf16[2048,1024]{1,0:T(8,128)(2,1)}, bf16[2048,1024]{1,0:T(8,128)(2,1)}, bf16[4,128,1024]{2,1,0:T(8,128)(2,1)}, bf16[2,2048,128]{2,1,0:T(8,128)...) custom-call(bf16[512,1024]{1,0:T(8,128)(2,1)} %fusion.3.n_hbm, f32[2048,128]{1,0:T(8,128)} %get-tuple-element.22.cos_ref, ...), custom_call_target="tpu_custom_call" | custom-call | flops 60000002048 | bytes 60000000 | tf_op jit(solution)/shard_map/pallas_call | solution.py:230
  115.1 360.3 %shard_map.101 = (f32[512,1024]{1,0:T(8,128)}, bf16[3072,1024]{1,0:T(8,128)(2,1)}, bf16[1024,1024]{1,0:T(8,128)(2,1)}) custom-call(bf16[2048,1024]{1,0:T(8,128)(2,1)} %get-tuple-element.12.nown_hbm, bf16[2048,1024]{1,0:T(8,128)(2,1)} %get-tuple-element.13.npar_hbm, bf16[4,128,1024]{2,1,0:T(8,128)(2,1)} %get-tuple-element.14.q_hbm, ...), custom_call_target="tpu_custom_call" | custom-call | flops 399999991808 | bytes 200000000 | tf_op jit(solution)/shard_map/pallas_call | solution.py:590
  475.4 3.2 fusion.4
  (4 shorter events, 0.0 us)

commit v3 on v2

--- a/solution.py
+++ b/solution.py
@@ -21,8 +21,8 @@
     return jnp.where(even, pltpu.roll(x, width - 1, 1), pltpu.roll(x, 1, 1))
 
 
-def qkv_kernel(nx, ny, n_hbm, cos_ref, sin_ref, wq, wk, wv, wg, wu, nown_out, npar_out, q_out, kv_out, wgp, wup,
-               nown, npar, wbuf, pbuf, sbuf, rbuf, qst, kv, in_sem, w_sem, ws_sem, wr_sem, ns_sem, nr_sem, ps_sem, pr_sem,
+def qkv_kernel(nx, ny, x_ref, gain_ref, cos_ref, sin_ref, wq, wk, wv, wg, wu, nown_out, npar_out, q_out, kv_out, wgp, wup,
+               nown, npar, wbuf, pbuf, sbuf, rbuf, qst, kv, stats, st_sem, sr_sem, in_sem, w_sem, ws_sem, wr_sem, ns_sem, nr_sem, ps_sem, pr_sem,
                send_sem, recv_sem, ks_sem, kr_sem, gs_sem, gr_sem):
     tokens, feats = nown.shape
     bt = tokens // ny
@@ -56,12 +56,10 @@
         return pltpu.make_async_remote_copy(src_ref=src, dst_ref=dst, send_sem=send, recv_sem=recv, device_id=device, device_id_type=MESH)
 
     barrier = pltpu.get_barrier_semaphore()
-    peers = [{"tx": partner}] + [{"tx": chip(i)} for i in range(1, nx)] + [{"ty": lax.rem(ty + k, ny)} for k in range(1, ny)]
+    group = nx * CORES
+    peers = [{"tx": lax.rem(tx + i, group)} for i in range(1, group)] + [{"ty": lax.rem(ty + k, ny)} for k in range(1, ny)]
     for peer in peers:
         pl.semaphore_signal(barrier, inc=1, device_id=peer, device_id_type=MESH)
-
-    load_n = pltpu.make_async_copy(n_hbm, nown.at[rows_of(0), :], in_sem.at[0])
-    load_n.start()
 
     def w_parts(c):
         parts = []
@@ -75,12 +73,36 @@
     local_w = [pltpu.make_async_copy(s, wbuf.at[d, pl.ds(0, feats), cols], w_sem.at[i]) for i, (s, d, cols) in enumerate(w_parts(core))]
     for copy in local_w:
         copy.start()
+
+    x_wide = x_ref[...].astype(F32)
+    part_mean = jnp.sum(x_wide, axis=1, keepdims=True) / feats
+    centred = x_wide - part_mean
+    lane = lax.broadcasted_iota(jnp.int32, (bt, HEAD), 1)
+    stats[tx] = jnp.where(lane == 0, part_mean, jnp.sum(centred * centred, axis=1, keepdims=True)).T[:8]
+
+    def stat_copy(i):
+        return remote(stats.at[tx], stats.at[tx], st_sem.at[i - 1], sr_sem.at[i - 1], {"tx": lax.rem(tx + i, group)})
+
+    def stat_arrival(i):
+        slot = stats.at[lax.rem(tx + group - i, group)]
+        return remote(slot, slot, st_sem.at[i - 1], sr_sem.at[i - 1], {"tx": lax.rem(tx + i, group)})
+
     pl.semaphore_wait(barrier, len(peers))
-    load_n.wait()
-
+    for i in range(1, group):
+        stat_copy(i).start()
     own = nown.at[rows_of(0), :]
     swap_w = [remote(s, wbuf.at[d, pl.ds(feats, feats), cols], ws_sem.at[i], wr_sem.at[i], {"tx": partner})
               for i, (s, d, cols) in enumerate(w_parts(1 - core))]
+    for copy in swap_w:
+        copy.start()
+    for i in range(1, group):
+        stat_arrival(i).wait_recv()
+    means = [stats[i, 0:1, :] for i in range(group)]
+    mean = sum(means) / group
+    var = sum(stats[i, 1:2, :] + feats * (means[i] - mean) * (means[i] - mean) for i in range(group)) / (feats * group)
+    sub = lax.broadcasted_iota(jnp.int32, (HEAD, bt), 0)
+    cols = jnp.where(sub == 0, mean, lax.rsqrt(var + 1e-5)).T
+    nown[rows_of(0), :] = (gain_ref[...] * (x_wide - cols[:, 0:1]) * cols[:, 1:2]).astype(BF16)
     to_south = remote(own, own, ns_sem.at[0], nr_sem.at[0], {"ty": south})
     to_north = remote(own, own, ns_sem.at[1], nr_sem.at[1], {"ty": north})
     to_south.start()
@@ -103,8 +125,6 @@
         return remote(nown.at[rows, :], nown.at[rows, :], ns_sem.at[i], nr_sem.at[i], {"ty": south if i == 0 else north})
 
     pair(0).start()
-    for copy in swap_w:
-        copy.start()
 
     piece = feats // ny
     goff = pl.multiple_of((1 - core) * half, 128)
@@ -134,61 +154,79 @@
         return (pltpu.make_async_copy(nown.at[rows, :], nown_out.at[rows, :], in_sem.at[1 + 2 * p]),
                 pltpu.make_async_copy(npar.at[rows, :], npar_out.at[rows, :], in_sem.at[2 + 2 * p]))
 
-    for t in range(ny + hops):
-        if t < ny:
-            if t == 1:
-                near_arrival(0).wait_recv()
-                far(0).start()
-                pair(1).start()
-                near_arrival(1).wait_recv()
-                far(1).start()
-                pair(2).start()
-            if t == 3:
-                far_arrival(0).wait_recv()
-                far_arrival(1).wait_recv()
-                pair(3).start()
-            pair(t).wait_recv()
-            for copy in n_store(t):
-                copy.start()
-            if t == 0:
-                for copy in local_w:
-                    copy.wait()
-                for copy in swap_w:
-                    copy.wait_recv()
-            rows = rows_of(order[t])
-
-            @pl.loop(0, 2)
-            def _(d):
-                pbuf[d, t % nx] = (jnp.dot(nown[rows, :], wbuf[d, :feats, :], preferred_element_type=F32)
-                                   + jnp.dot(npar[rows, :], wbuf[d, feats:, :], preferred_element_type=F32))
-            for d in range(2):
-                sbuf[d, 0, t] = pbuf[d, t % nx, owner_rows(d, 0), :].astype(BF16)
-                hop(0, d, t).start()
-            for copy in swap_mlp(t):
-                copy.start()
-        for k in range(1, hops + 1):
-            p = t - k
-            if 0 <= p < ny:
-                for d in range(2):
-                    hop(k - 1, d, p).wait_recv()
-                    part = pbuf[d, p % nx, owner_rows(d, k), :] + rbuf[d, k - 1, p].astype(F32)
-                    if k < hops:
-                        sbuf[d, k, p] = part.astype(BF16)
-                        hop(k, d, p).start()
-                        continue
-                    rows = kv_rows(p)
-                    block = lax.rem(ty + order[p], ny)
-                    part = part.astype(BF16).astype(F32)
-                    cos, sin = cos_ref[rows, :], sin_ref[rows, :]
-                    small = part[:, qcols:]
-                    if d == 0:
-                        small = small * cos + swap_lanes(small) * sin
-                    kv[d, rows, :] = small.astype(BF16)
-                    for i in range(1, nx):
-                        kv_copy(d, p, i).start()
-                    for h in range(qcols // HEAD):
-                        head = part[:, h * HEAD:(h + 1) * HEAD]
-                        qst[block, :, d * qcols + h * HEAD:d * qcols + (h + 1) * HEAD] = (head * cos + swap_lanes(head) * sin).astype(BF16)
+    def product(p):
+        pair(p).wait_recv()
+        for copy in n_store(p):
+            copy.start()
+        rows = rows_of(order[p])
+
+        @pl.loop(0, 2)
+        def _(d):
+            pbuf[d, p] = (jnp.dot(nown[rows, :], wbuf[d, :feats, :], preferred_element_type=F32)
+                          + jnp.dot(npar[rows, :], wbuf[d, feats:, :], preferred_element_type=F32))
+        for d in range(2):
+            sbuf[d, 0, p] = pbuf[d, p, owner_rows(d, 0), :].astype(BF16)
+            hop(0, d, p).start()
+
+    def reduce(k, p):
+        for d in range(2):
+            hop(k - 1, d, p).wait_recv()
+            part = pbuf[d, p, owner_rows(d, k), :] + rbuf[d, k - 1, p].astype(F32)
+            if k < hops:
+                sbuf[d, k, p] = part.astype(BF16)
+                hop(k, d, p).start()
+                continue
+            rows = kv_rows(p)
+            block = lax.rem(ty + order[p], ny)
+            part = part.astype(BF16).astype(F32)
+            cos, sin = cos_ref[block], sin_ref[block]
+            small = part[:, qcols:]
+            if d == 0:
+                small = small * cos + swap_lanes(small) * sin
+            kv[d, rows, :] = small.astype(BF16)
+            for i in range(1, nx):
+                kv_copy(d, p, i).start()
+            for h in range(qcols // HEAD):
+                head = part[:, h * HEAD:(h + 1) * HEAD]
+                qst[block, :, d * qcols + h * HEAD:d * qcols + (h + 1) * HEAD] = (head * cos + swap_lanes(head) * sin).astype(BF16)
+
+    def give(i):
+        for copy in swap_mlp(i):
+            copy.start()
+
+    for copy in local_w:
+        copy.wait()
+    for copy in swap_w:
+        copy.wait_recv()
+    product(0)
+    give(0)
+    give(1)
+    reduce(1, 0)
+    give(2)
+    reduce(2, 0)
+    near_arrival(0).wait_recv()
+    far(0).start()
+    pair(1).start()
+    near_arrival(1).wait_recv()
+    far(1).start()
+    pair(2).start()
+    reduce(3, 0)
+    product(1)
+    product(2)
+    reduce(1, 1)
+    reduce(1, 2)
+    far_arrival(0).wait_recv()
+    far_arrival(1).wait_recv()
+    pair(3).start()
+    reduce(2, 1)
+    reduce(2, 2)
+    product(3)
+    give(3)
+    reduce(3, 1)
+    reduce(3, 2)
+    reduce(1, 3)
+    reduce(2, 3)
+    reduce(3, 3)
 
     for p in range(ny):
         for d in range(2):
@@ -204,6 +242,8 @@
             copy.wait()
     for copy in swap_w:
         copy.wait_send()
+    for i in range(1, group):
+        stat_copy(i).wait_send()
     to_south.wait_send()
     to_north.wait_send()
     far(0).wait_send()
@@ -215,8 +255,8 @@
         copy.wait()
 
 
-def qkv_ring(n_blk, cos, sin, wq, wk, wv, wg, wu, nx, ny):
-    bt, feats = n_blk.shape
+def qkv_ring(x_blk, gain, cos, sin, wq, wk, wv, wg, wu, nx, ny):
+    bt, feats = x_blk.shape
     tokens = bt * ny
     ob = bt // nx
     half = wg.shape[1] // CORES
@@ -231,19 +271,20 @@
         functools.partial(qkv_kernel, nx, ny),
         out_shape=(sds((tokens, feats), BF16), sds((tokens, feats), BF16), sds((ny, ob, qhalf), BF16), sds((2, tokens, HEAD), BF16),
                    sds((feats, half), BF16), sds((feats, half), BF16)),
-        in_specs=[any_spec, vmem, vmem] + [any_spec] * 5, out_specs=[any_spec] * 6,
+        in_specs=[vmem] * 4 + [any_spec] * 5, out_specs=[any_spec] * 6,
         scratch_shapes=[
             pltpu.VMEM((tokens, feats), BF16), pltpu.VMEM((tokens, feats), BF16),
             pltpu.VMEM((2, 2 * feats, cols), BF16),
             pltpu.VMEM((2, nx, bt, cols), F32),
             pltpu.VMEM((2, hops, ny, ob, cols), BF16), pltpu.VMEM((2, hops, ny, ob, cols), BF16),
             pltpu.VMEM((ny, ob, qhalf), BF16), pltpu.VMEM((2, tokens, HEAD), BF16),
+            pltpu.VMEM((nx * CORES, 8, bt), F32), dma((nx * CORES - 1,)), dma((nx * CORES - 1,)),
             dma((1 + 2 * ny,)), dma((4,)), dma((4,)), dma((4,)), dma((4,)), dma((4,)), dma((ny,)), dma((ny,)),
             dma((2, hops, ny)), dma((2, hops, ny)), dma((2, ny, hops)), dma((2, ny, hops)), dma((2, ny)), dma((2, ny)),
         ],
         compiler_params=pltpu.CompilerParams(collective_id=0, has_side_effects=True, vmem_limit_bytes=60 << 20),
         cost_estimate=pl.CostEstimate(flops=60_000_000_000, bytes_accessed=60_000_000, transcendentals=0),
-    )(n_blk, cos, sin, wq, wk, wv, wg, wu)
+    )(x_blk, gain, cos, sin, wq, wk, wv, wg, wu)
 
 
 SLOTS = 3
@@ -379,18 +420,13 @@
     start(n_copies(0))
     for d in range(2):
         start(w_copies(0, d))
-    for p in range(1, ny):
-        start(n_copies(p))
     loads = (pltpu.make_async_copy(q_hbm, qst, in_sem.at[0]), pltpu.make_async_copy(kv_hbm, kv, in_sem.at[1]))
-    start(loads)
     pl.semaphore_wait(barrier, len(peers))
     swaps = []
     for i, (src, dst, size) in enumerate(((wd, wdp, half), (wo, wop, ahalf))):
         rows = pl.ds(pl.multiple_of((1 - core) * size, width), size)
         swaps.append(pltpu.make_async_remote_copy(src_ref=src.at[rows, :], dst_ref=dst, send_sem=gs_sem.at[i], recv_sem=gr_sem.at[i],
                                                   device_id={"tx": partner}, device_id_type=MESH))
-    start(swaps)
-    wait(loads)
 
     def attention(p):
         block = lax.rem(ty + 1 + p, ny)
@@ -463,6 +499,13 @@
                 sbuf[d, 0, lax.rem(t, SLOTS)] = pbuf[d, pslot, owner_rows(d, 0), :].astype(BF16)
                 hop(0, d, t).start()
 
+        @pl.when(t == 1)
+        def _():
+            start(swaps)
+            start(loads)
+            for p in range(1, ny):
+                start(n_copies(p))
+
         for k in range(1, last_hop + 1):
             @pl.when(reduces(t - k))
             def _():
@@ -558,6 +601,9 @@
 
         @pl.when(jnp.logical_and(t < total, lax.rem(t, chunks) == chunks // 2))
         def _():
+            @pl.when(t < chunks)
+            def _():
+                wait(loads)
             attention(t // chunks)
 
         @pl.when(jnp.logical_and(t >= 1, t < signal_end))
@@ -621,20 +667,16 @@
     nx = tx_size // CORES
 
     def per_device(x_blk, positions, norm_gain, w_q, w_k, w_v, w_o, w_gate, w_up, w_down):
-        d_model = x_blk.shape[1] * tx_size
         seq_len = positions.shape[1]
         inv_freq = ROPE_THETA ** (-2.0 * (jnp.arange(HEAD) // 2).astype(F32) / HEAD)
-        angle = positions.reshape(-1).astype(F32)[:, None] * inv_freq[None, :]
+        own_pos = positions.reshape(ty_size, nx, -1)
+        own_pos = lax.dynamic_index_in_dim(own_pos, lax.axis_index("tx") // CORES, 1, keepdims=False)
+        angle = own_pos.astype(F32)[:, :, None] * inv_freq
         cos = jnp.cos(angle)
         sin = jnp.sin(angle) * jnp.where(jnp.arange(HEAD) % 2 == 0, -1.0, 1.0).astype(F32)
-        x_wide = x_blk.astype(F32)
-        tok_stats = lax.psum(jnp.stack([jnp.sum(x_wide, axis=1), jnp.sum(x_wide * x_wide, axis=1)], axis=1), "tx")
-        tok_mean = tok_stats[:, :1] / d_model
-        tok_var = tok_stats[:, 1:] / d_model - tok_mean * tok_mean
-        normed = (norm_gain * (x_wide - tok_mean) * lax.rsqrt(tok_var + 1e-5)).astype(BF16)
-        n_own, n_par, q, kv, wgp, wup = qkv_ring(normed, cos, sin, w_q, w_k, w_v, w_gate, w_up, nx, ty_size)
+        n_own, n_par, q, kv, wgp, wup = qkv_ring(x_blk, norm_gain[None, :], cos, sin, w_q, w_k, w_v, w_gate, w_up, nx, ty_size)
         block_sum, _, _ = mlp_ring(n_own, n_par, q, kv, w_gate, w_up, wgp, wup, w_down, w_o, nx, ty_size, 256, seq_len)
-        return (x_wide + block_sum).astype(BF16)
+        return (x_blk.astype(F32) + block_sum).astype(BF16)
 
     in_specs = (P(("dp", "ty"), "tx"), P("dp", None), P("tx"), P("tx", "ty"), P("tx", "ty"), P("tx", "ty"),
                 P("ty", "tx"), P("tx", "ty"), P("tx", "ty"), P("ty", "tx"))

time: 479 us -> 455 us (0.950)
  blocking collectives: 13.9 us -> 0 us
  other arithmetic: 13.7 us -> 5.01 us
    psum x1 -> x0, blocking collectives: 13.9 us -> none  [per_device(): lax.psum(jnp.stack([jnp.sum(x_wide, axis=1), jnp.sum(x_wide * x_wide, axi...]
where the time goes in v3:
time: 455 us
  Pallas kernels  449 us (99%)
  other arithmetic  5.01 us (1%)
    pallas_call x1, Pallas kernels, mlp_ring(): pl.pallas_call(functools.partial(mlp_kernel, nx, ny, width, seq_len), out...  358 us
    pallas_call x1, Pallas kernels, qkv_ring(): pl.pallas_call(functools.partial(qkv_kernel, nx, ny), out_shape=(sds((tok...  91.3 us

profile of v3, /device:TPU:97, one launch (start us, length us, event | category | flops | bytes accessed | tf_op | source)
XLA Modules:
  0.0 454.9 jit_solution(4304885053002105813)
XLA Ops:
  0.0 0.7 reshape.36
  0.8 1.8 fusion
  2.6 91.3 %shard_map.100 = (bf16[2048,1024]{1,0:T(8,128)(2,1)}, bf16[2048,1024]{1,0:T(8,128)(2,1)}, bf16[4,128,1024]{2,1,0:T(8,128)(2,1)}, bf16[2,2048,128]{2,1,0:T(8,128)...) custom-call(bf16[512,1024]{1,0:T(8,128)(2,1)} %x_ref.1, f32[1,1024]{1,0:T(1,128)} %bitcast.5, ...), custom_call_target="tpu_custom_call" | custom-call | flops 60000002048 | bytes 60000000 | tf_op jit(solution)/shard_map/pallas_call | solution.py:270
  93.9 357.8 %shard_map.101 = (f32[512,1024]{1,0:T(8,128)}, bf16[3072,1024]{1,0:T(8,128)(2,1)}, bf16[1024,1024]{1,0:T(8,128)(2,1)}) custom-call(bf16[2048,1024]{1,0:T(8,128)(2,1)} %get-tuple-element.12.nown_hbm, bf16[2048,1024]{1,0:T(8,128)(2,1)} %get-tuple-element.13.npar_hbm, bf16[4,128,1024]{2,1,0:T(8,128)(2,1)} %get-tuple-element.14.q_hbm, ...), custom_call_target="tpu_custom_call" | custom-call | flops 399999991808 | bytes 200000000 | tf_op jit(solution)/shard_map/pallas_call | solution.py:636
  451.7 3.2 add_convert_fusion
  (3 shorter events, 0.0 us)

commit v4 on v3

--- a/solution.py
+++ b/solution.py
@@ -10,6 +10,8 @@
 WINDOW = 4096
 ROPE_THETA = 50000
 CORES = 2
+WIDTH = 256
+EARLY = 3
 MESH = pl.DeviceIdType.MESH
 F32 = jnp.float32
 BF16 = jnp.bfloat16
@@ -21,8 +23,8 @@
     return jnp.where(even, pltpu.roll(x, width - 1, 1), pltpu.roll(x, 1, 1))
 
 
-def qkv_kernel(nx, ny, x_ref, gain_ref, cos_ref, sin_ref, wq, wk, wv, wg, wu, nown_out, npar_out, q_out, kv_out, wgp, wup,
-               nown, npar, wbuf, pbuf, sbuf, rbuf, qst, kv, stats, st_sem, sr_sem, in_sem, w_sem, ws_sem, wr_sem, ns_sem, nr_sem, ps_sem, pr_sem,
+def qkv_kernel(nx, ny, x_ref, gain_ref, cos_ref, sin_ref, wq, wk, wv, wg, wu, nown_out, npar_out, q_out, kv_out, wgp, wup, h_out,
+               nown, npar, wbuf, pbuf, sbuf, rbuf, qst, kv, wm, pm, sm, rm, hst, wl_sem, wms_sem, wmr_sem, ms_sem, mr_sem, stats, st_sem, sr_sem, in_sem, w_sem, ws_sem, wr_sem, ns_sem, nr_sem, ps_sem, pr_sem,
                send_sem, recv_sem, ks_sem, kr_sem, gs_sem, gr_sem):
     tokens, feats = nown.shape
     bt = tokens // ny
@@ -69,6 +71,12 @@
             parts.append((wq.at[:, col], d, pl.ds(0, qcols)))
             parts.append(((wk if d == 0 else wv).at[:, small], d, pl.ds(qcols, HEAD)))
         return parts
+
+    def early_parts(c, m):
+        for d in range(2):
+            col = pl.ds(pl.multiple_of(c * half + d * (half // 2) + m * WIDTH, WIDTH), WIDTH)
+            for i, src in enumerate((wg, wu)):
+                yield src.at[:, col], d, i, pl.ds(i * WIDTH, WIDTH)
 
     local_w = [pltpu.make_async_copy(s, wbuf.at[d, pl.ds(0, feats), cols], w_sem.at[i]) for i, (s, d, cols) in enumerate(w_parts(core))]
     for copy in local_w:
@@ -108,6 +116,11 @@
     to_south.start()
     to_north.start()
 
+    early_local = [[pltpu.make_async_copy(src, wm.at[d, m, pl.ds(0, feats), cols], wl_sem.at[m, d, i])
+                    for src, d, i, cols in early_parts(core, m)] for m in range(EARLY)]
+    early_swap = [[remote(src, wm.at[d, m, pl.ds(feats, feats), cols], wms_sem.at[m, d, i], wmr_sem.at[m, d, i], {"tx": partner})
+                   for src, d, i, cols in early_parts(1 - core, m)] for m in range(EARLY)]
+
     def pair(p):
         rows = rows_of(order[p])
         return remote(nown.at[rows, :], npar.at[rows, :], ps_sem.at[p], pr_sem.at[p], {"tx": partner})
@@ -125,6 +138,9 @@
         return remote(nown.at[rows, :], nown.at[rows, :], ns_sem.at[i], nr_sem.at[i], {"ty": south if i == 0 else north})
 
     pair(0).start()
+    for m in range(EARLY):
+        for copy in early_local[m] + early_swap[m]:
+            copy.start()
 
     piece = feats // ny
     goff = pl.multiple_of((1 - core) * half, 128)
@@ -194,27 +210,69 @@
         for copy in swap_mlp(i):
             copy.start()
 
+    def early_hop(k, d, m):
+        target = chip(1 if d == 0 else nx - 1)
+        return remote(sm.at[d, k, m], rm.at[d, k, m], ms_sem.at[d, k, m], mr_sem.at[d, k, m], {"tx": target})
+
+    def early_product(m):
+        for copy in early_local[m]:
+            copy.wait()
+        for copy in early_swap[m]:
+            copy.wait_recv()
+        rows = rows_of(0)
+
+        @pl.loop(0, 2)
+        def _(d):
+            pm[d, m] = (jnp.dot(nown[rows, :], wm[d, m, :feats, :], preferred_element_type=F32)
+                        + jnp.dot(npar[rows, :], wm[d, m, feats:, :], preferred_element_type=F32))
+        for d in range(2):
+            sm[d, 0, m] = pm[d, m, owner_rows(d, 0), :].astype(BF16)
+            early_hop(0, d, m).start()
+
+    def early_reduce(k, m):
+        for d in range(2):
+            early_hop(k - 1, d, m).wait_recv()
+            part = pm[d, m, owner_rows(d, k), :] + rm[d, k - 1, m].astype(F32)
+            if k < hops:
+                sm[d, k, m] = part.astype(BF16)
+                early_hop(k, d, m).start()
+            else:
+                gate = part[:, :WIDTH].astype(BF16).astype(F32)
+                up = part[:, WIDTH:].astype(BF16).astype(F32)
+                hst[d, m] = (gate * jax.nn.sigmoid(gate) * up).astype(BF16)
+
+    def later(step, *args):
+        if args[-1] < EARLY:
+            step(*args)
+
     for copy in local_w:
         copy.wait()
     for copy in swap_w:
         copy.wait_recv()
     product(0)
+    early_product(0)
     give(0)
-    give(1)
     reduce(1, 0)
-    give(2)
+    later(early_product, 1)
     reduce(2, 0)
+    early_reduce(1, 0)
+    reduce(3, 0)
+    later(early_reduce, 1, 1)
     near_arrival(0).wait_recv()
     far(0).start()
     pair(1).start()
     near_arrival(1).wait_recv()
     far(1).start()
     pair(2).start()
-    reduce(3, 0)
+    early_reduce(2, 0)
     product(1)
     product(2)
+    give(1)
+    give(2)
+    later(early_reduce, 2, 1)
     reduce(1, 1)
     reduce(1, 2)
+    early_reduce(3, 0)
     far_arrival(0).wait_recv()
     far_arrival(1).wait_recv()
     pair(3).start()
@@ -222,11 +280,16 @@
     reduce(2, 2)
     product(3)
     give(3)
+    later(early_product, 2)
+    later(early_reduce, 3, 1)
     reduce(3, 1)
     reduce(3, 2)
     reduce(1, 3)
+    later(early_reduce, 1, 2)
     reduce(2, 3)
+    later(early_reduce, 2, 2)
     reduce(3, 3)
+    later(early_reduce, 3, 2)
 
     for p in range(ny):
         for d in range(2):
@@ -242,13 +305,20 @@
             copy.wait()
     for copy in swap_w:
         copy.wait_send()
+    for m in range(EARLY):
+        for copy in early_swap[m]:
+            copy.wait_send()
+        for d in range(2):
+            for k in range(hops):
+                early_hop(k, d, m).wait_send()
     for i in range(1, group):
         stat_copy(i).wait_send()
     to_south.wait_send()
     to_north.wait_send()
     far(0).wait_send()
     far(1).wait_send()
-    stores = (pltpu.make_async_copy(qst, q_out, in_sem.at[0]), pltpu.make_async_copy(kv, kv_out, in_sem.at[1]))
+    stores = (pltpu.make_async_copy(qst, q_out, in_sem.at[0]), pltpu.make_async_copy(kv, kv_out, in_sem.at[1]),
+              pltpu.make_async_copy(hst, h_out, in_sem.at[2]))
     for copy in stores:
         copy.start()
     for copy in stores:
@@ -270,19 +340,23 @@
     return pl.pallas_call(
         functools.partial(qkv_kernel, nx, ny),
         out_shape=(sds((tokens, feats), BF16), sds((tokens, feats), BF16), sds((ny, ob, qhalf), BF16), sds((2, tokens, HEAD), BF16),
-                   sds((feats, half), BF16), sds((feats, half), BF16)),
-        in_specs=[vmem] * 4 + [any_spec] * 5, out_specs=[any_spec] * 6,
+                   sds((feats, half), BF16), sds((feats, half), BF16), sds((2, EARLY, ob, WIDTH), BF16)),
+        in_specs=[vmem] * 4 + [any_spec] * 5, out_specs=[any_spec] * 7,
         scratch_shapes=[
             pltpu.VMEM((tokens, feats), BF16), pltpu.VMEM((tokens, feats), BF16),
             pltpu.VMEM((2, 2 * feats, cols), BF16),
             pltpu.VMEM((2, nx, bt, cols), F32),
             pltpu.VMEM((2, hops, ny, ob, cols), BF16), pltpu.VMEM((2, hops, ny, ob, cols), BF16),
             pltpu.VMEM((ny, ob, qhalf), BF16), pltpu.VMEM((2, tokens, HEAD), BF16),
+            pltpu.VMEM((2, EARLY, 2 * feats, 2 * WIDTH), BF16), pltpu.VMEM((2, EARLY, bt, 2 * WIDTH), F32),
+            pltpu.VMEM((2, hops, EARLY, ob, 2 * WIDTH), BF16), pltpu.VMEM((2, hops, EARLY, ob, 2 * WIDTH), BF16),
+            pltpu.VMEM((2, EARLY, ob, WIDTH), BF16),
+            dma((EARLY, 2, 2)), dma((EARLY, 2, 2)), dma((EARLY, 2, 2)), dma((2, hops, EARLY)), dma((2, hops, EARLY)),
             pltpu.VMEM((nx * CORES, 8, bt), F32), dma((nx * CORES - 1,)), dma((nx * CORES - 1,)),
             dma((1 + 2 * ny,)), dma((4,)), dma((4,)), dma((4,)), dma((4,)), dma((4,)), dma((ny,)), dma((ny,)),
             dma((2, hops, ny)), dma((2, hops, ny)), dma((2, ny, hops)), dma((2, ny, hops)), dma((2, ny)), dma((2, ny)),
         ],
-        compiler_params=pltpu.CompilerParams(collective_id=0, has_side_effects=True, vmem_limit_bytes=60 << 20),
+        compiler_params=pltpu.CompilerParams(collective_id=0, has_side_effects=True, vmem_limit_bytes=67043328),
         cost_estimate=pl.CostEstimate(flops=60_000_000_000, bytes_accessed=60_000_000, transcendentals=0),
     )(x_blk, gain, cos, sin, wq, wk, wv, wg, wu)
 
@@ -291,8 +365,8 @@
 HSLOTS = 8
 
 
-def mlp_kernel(nx, ny, width, seq_len, nown_hbm, npar_hbm, q_hbm, kv_hbm, wg, wu, wgp, wup, wd, wo, out_ref, wdp, wop,
-               nown, npar, wbuf, w2buf, pbuf, sbuf, rbuf, hid, acc, xrecv, ysend, yrecv, qst, kv, abuf,
+def mlp_kernel(nx, ny, width, seq_len, nown_hbm, npar_hbm, q_hbm, kv_hbm, h_hbm, wg, wu, wgp, wup, wd, wo, out_ref, wdp, wop,
+               nown, npar, wbuf, w2buf, pbuf, sbuf, rbuf, hid, acc, xrecv, ysend, yrecv, qst, kv, abuf, hst,
                in_sem, n_sem, w_sem, w2_sem, send_sem, recv_sem, xs_sem, xr_sem, ys_sem, yr_sem, gs_sem, gr_sem, credit, xcredit):
     tokens, feats = nown.shape
     bt = tokens // ny
@@ -410,7 +484,8 @@
         return lax.rem(q, chunks) < mlp_chunks
 
     def reduces(q):
-        return jnp.logical_and(valid(q), is_mlp(q))
+        early = jnp.logical_and(q >= total - chunks, q < total - chunks + EARLY)
+        return jnp.logical_and(jnp.logical_and(valid(q), is_mlp(q)), jnp.logical_not(early))
 
     def n_copies(p):
         rows = block_rows(p)
@@ -420,7 +495,8 @@
     start(n_copies(0))
     for d in range(2):
         start(w_copies(0, d))
-    loads = (pltpu.make_async_copy(q_hbm, qst, in_sem.at[0]), pltpu.make_async_copy(kv_hbm, kv, in_sem.at[1]))
+    loads = (pltpu.make_async_copy(q_hbm, qst, in_sem.at[0]), pltpu.make_async_copy(kv_hbm, kv, in_sem.at[1]),
+             pltpu.make_async_copy(h_hbm, hst, in_sem.at[2]))
     pl.semaphore_wait(barrier, len(peers))
     swaps = []
     for i, (src, dst, size) in enumerate(((wd, wdp, half), (wo, wop, ahalf))):
@@ -478,14 +554,14 @@
             for d in range(2):
                 start(w_copies(t + 1, d))
 
+        @pl.when(jnp.logical_and(t < total, lax.rem(t, chunks) == 0))
+        def _():
+            wait(n_copies(t // chunks))
+
         @pl.when(reduces(t))
         def _():
             for d in range(2):
                 wait(w_copies(t, d))
-
-            @pl.when(lax.rem(t, chunks) == 0)
-            def _():
-                wait(n_copies(t // chunks))
 
             rows = block_rows(t // chunks)
             slot = lax.rem(t, 2)
@@ -522,6 +598,13 @@
                         hid[d, hslot, gather_rows(d, 0), :] = (gate * jax.nn.sigmoid(gate) * up).astype(BF16)
                     hop(k, d, t).start()
 
+        for i in range(EARLY):
+            @pl.when(t - last_hop == total - chunks + i)
+            def _():
+                for d in range(2):
+                    hid[d, lax.rem(t - last_hop + HSLOTS, HSLOTS), gather_rows(d, 0), :] = hst[d, i]
+                    hop(last_hop, d, t).start()
+
         for i in range(adir // width):
             q = t - last_hop
 
@@ -622,7 +705,7 @@
     store.wait()
 
 
-def mlp_ring(n_own, n_par, q, kv, wg, wu, wgp, wup, wd, wo, nx, ny, width, seq_len):
+def mlp_ring(n_own, n_par, q, kv, early, wg, wu, wgp, wup, wd, wo, nx, ny, width, seq_len):
     tokens, feats = n_own.shape
     bt = tokens // ny
     ob = bt // nx
@@ -636,7 +719,7 @@
     return pl.pallas_call(
         functools.partial(mlp_kernel, nx, ny, width, seq_len),
         out_shape=(sds((bt, cols), F32), sds((half, cols), BF16), sds((ahalf, cols), BF16)),
-        in_specs=[any_spec] * 10, out_specs=[any_spec] * 3,
+        in_specs=[any_spec] * 11, out_specs=[any_spec] * 3,
         scratch_shapes=[
             pltpu.VMEM((tokens, feats), BF16),
             pltpu.VMEM((tokens, feats), BF16),
@@ -650,15 +733,15 @@
             pltpu.VMEM((bt, cols), F32),
             pltpu.VMEM((ny - 1, bt, cols), BF16),
             pltpu.VMEM((ny - 1, bt, cols), BF16),
-            pltpu.VMEM(q.shape, BF16), pltpu.VMEM(kv.shape, BF16), pltpu.VMEM((ob, ahalf), BF16),
-            dma((2,)), dma((2, ny)), dma((2, 2, 4)), dma((2, 2, 2)),
+            pltpu.VMEM(q.shape, BF16), pltpu.VMEM(kv.shape, BF16), pltpu.VMEM((ob, ahalf), BF16), pltpu.VMEM(early.shape, BF16),
+            dma((3,)), dma((2, ny)), dma((2, 2, 4)), dma((2, 2, 2)),
             dma((2, kinds, SLOTS)), dma((2, kinds, SLOTS)),
             dma, dma, dma((ny - 1,)), dma((ny - 1,)), dma((2,)), dma((2,)),
             pltpu.SemaphoreType.REGULAR((2,)), pltpu.SemaphoreType.REGULAR,
         ],
         compiler_params=pltpu.CompilerParams(collective_id=1, has_side_effects=True, vmem_limit_bytes=67043328),
         cost_estimate=pl.CostEstimate(flops=400_000_000_000, bytes_accessed=200_000_000, transcendentals=0),
-    )(n_own, n_par, q, kv, wg, wu, wgp, wup, wd, wo)
+    )(n_own, n_par, q, kv, early, wg, wu, wgp, wup, wd, wo)
 
 
 def solution(mesh):
@@ -674,8 +757,8 @@
         angle = own_pos.astype(F32)[:, :, None] * inv_freq
         cos = jnp.cos(angle)
         sin = jnp.sin(angle) * jnp.where(jnp.arange(HEAD) % 2 == 0, -1.0, 1.0).astype(F32)
-        n_own, n_par, q, kv, wgp, wup = qkv_ring(x_blk, norm_gain[None, :], cos, sin, w_q, w_k, w_v, w_gate, w_up, nx, ty_size)
-        block_sum, _, _ = mlp_ring(n_own, n_par, q, kv, w_gate, w_up, wgp, wup, w_down, w_o, nx, ty_size, 256, seq_len)
+        n_own, n_par, q, kv, wgp, wup, early = qkv_ring(x_blk, norm_gain[None, :], cos, sin, w_q, w_k, w_v, w_gate, w_up, nx, ty_size)
+        block_sum, _, _ = mlp_ring(n_own, n_par, q, kv, early, w_gate, w_up, wgp, wup, w_down, w_o, nx, ty_size, WIDTH, seq_len)
         return (x_blk.astype(F32) + block_sum).astype(BF16)
 
     in_specs = (P(("dp", "ty"), "tx"), P("dp", None), P("tx"), P("tx", "ty"), P("tx", "ty"), P("tx", "ty"),

time: 455 us -> 444 us (0.976)
  Pallas kernels: 449 us -> 438 us
    pallas_call x1, Pallas kernels: 358 us -> 335 us  [mlp_ring(): pl.pallas_call(functools.partial(mlp_kernel, nx, ny, width, seq_len), out...]
    pallas_call x1, Pallas kernels: 91.3 us -> 103 us  [qkv_ring(): pl.pallas_call(functools.partial(qkv_kernel, nx, ny), out_shape=(sds((tok...]
where the time goes in v4:
time: 444 us
  Pallas kernels  438 us (99%)
  other arithmetic  5.01 us (1%)
    pallas_call x1, Pallas kernels, mlp_ring(): pl.pallas_call(functools.partial(mlp_kernel, nx, ny, width, seq_len), out...  335 us
    pallas_call x1, Pallas kernels, qkv_ring(): pl.pallas_call(functools.partial(qkv_kernel, nx, ny), out_shape=(sds((tok...  103 us

profile of v4, /device:TPU:97, one launch (start us, length us, event | category | flops | bytes accessed | tf_op | source)
XLA Modules:
  0.0 443.9 jit_solution(12552146479983621503)
XLA Ops:
  0.0 0.7 reshape.36
  0.8 1.8 fusion
  2.6 103.0 %shard_map.100 = (bf16[2048,1024]{1,0:T(8,128)(2,1)}, bf16[2048,1024]{1,0:T(8,128)(2,1)}, bf16[4,128,1024]{2,1,0:T(8,128)(2,1)}, bf16[2,2048,128]{2,1,0:T(8,128)...) custom-call(bf16[512,1024]{1,0:T(8,128)(2,1)} %x_ref.1, ...), custom_call_target="tpu_custom_call" | custom-call | flops 60000002048 | bytes 60000000 | tf_op jit(solution)/shard_map/pallas_call | solution.py:340
  105.5 335.2 %shard_map.101 = (f32[512,1024]{1,0:T(8,128)}, bf16[3072,1024]{1,0:T(8,128)(2,1)}, bf16[1024,1024]{1,0:T(8,128)(2,1)}) custom-call(bf16[2048,1024]{1,0:T(8,128)(2,1)} %get-tuple-element.13.nown_hbm, bf16[2048,1024]{1,0:T(8,128)(2,1)} %get-tuple-element.14.npar_hbm, bf16[4,128,1024]{2,1,0:T(8,128)(2,1)} %get-tuple-element.15.q_hbm, ...), custom_call_target="tpu_custom_call" | custom-call | flops 399999991808 | bytes 200000000 | tf_op jit(solution)/shard_map/pallas_call | solution.py:719
  440.8 3.2 add_convert_fusion
  (3 shorter events, 0.0 us)

commit v5 on v4

--- a/solution.py
+++ b/solution.py
@@ -256,7 +256,6 @@
     later(early_product, 1)
     reduce(2, 0)
     early_reduce(1, 0)
-    reduce(3, 0)
     later(early_reduce, 1, 1)
     near_arrival(0).wait_recv()
     far(0).start()
@@ -265,6 +264,7 @@
     far(1).start()
     pair(2).start()
     early_reduce(2, 0)
+    reduce(3, 0)
     product(1)
     product(2)
     give(1)

time: 444 us -> 445 us (level)
  no operation moved by 1% of the time
where the time goes in v5:
time: 445 us; the launch traced here: 444 us
  Pallas kernels  439 us (99%)
  other arithmetic  5.01 us (1%)
    pallas_call x1, Pallas kernels, mlp_ring(): pl.pallas_call(functools.partial(mlp_kernel, nx, ny, width, seq_len), out...  336 us
    pallas_call x1, Pallas kernels, qkv_ring(): pl.pallas_call(functools.partial(qkv_kernel, nx, ny), out_shape=(sds((tok...  103 us

profile of v5, /device:TPU:97, one launch (start us, length us, event | category | flops | bytes accessed | tf_op | source)
XLA Modules:
  0.0 444.5 jit_solution(6901755219578320692)
XLA Ops:
  0.0 0.7 reshape.36
  0.8 1.8 fusion
  2.6 103.0 %shard_map.100 = (bf16[2048,1024]{1,0:T(8,128)(2,1)}, bf16[2048,1024]{1,0:T(8,128)(2,1)}, bf16[4,128,1024]{2,1,0:T(8,128)(2,1)}, bf16[2,2048,128]{2,1,0:T(8,128)...) custom-call(bf16[512,1024]{1,0:T(8,128)(2,1)} %x_ref.1, ...), custom_call_target="tpu_custom_call" | custom-call | flops 60000002048 | bytes 60000000 | tf_op jit(solution)/shard_map/pallas_call | solution.py:340
  105.5 335.7 %shard_map.101 = (f32[512,1024]{1,0:T(8,128)}, bf16[3072,1024]{1,0:T(8,128)(2,1)}, bf16[1024,1024]{1,0:T(8,128)(2,1)}) custom-call(bf16[2048,1024]{1,0:T(8,128)(2,1)} %get-tuple-element.13.nown_hbm, bf16[2048,1024]{1,0:T(8,128)(2,1)} %get-tuple-element.14.npar_hbm, bf16[4,128,1024]{2,1,0:T(8,128)(2,1)} %get-tuple-element.15.q_hbm, ...), custom_call_target="tpu_custom_call" | custom-call | flops 399999991808 | bytes 200000000 | tf_op jit(solution)/shard_map/pallas_call | solution.py:719
  441.3 3.2 add_convert_fusion
  (3 shorter events, 0.0 us)
